TPU v7x, 32 devices: a whole 2x2x4 slice. The times are simulated.
32 devices in a mesh: blk: 16 (over z, y, core), head: 2 (over x).
Axes of the slice: x: 2, y: 2, z: 4, core: 2. Of those that a mesh axis runs over, the one named last changes fastest.
Arguments:
- tokens: bfloat16 [2048, 3584], P(('blk', 'head')), may hold values from -100 to 100
- norm_gain: float32 [3584], replicated, may hold values from 0.1 to 1.9
- w_query: bfloat16 [3584, 3072], P('blk', 'head'), may hold values from -0.09375 to 0.09375
- w_key: bfloat16 [3584, 512], P('blk'), may hold values from -0.09375 to 0.09375
- w_value: bfloat16 [3584, 512], P('blk'), may hold values from -0.09375 to 0.09375
- q_bias: float32 [3072], P('head'), may hold values from -200 to 200
- k_bias: float32 [512], replicated, may hold values from -25 to 25
- v_bias: float32 [512], replicated, may hold values from -2.5 to 2.5
- w_out: bfloat16 [3072, 3584], P('head', 'blk'), may hold values from -0.109375 to 0.109375
Outputs:
- attention_out: bfloat16 [2048, 3584], P(('blk', 'head'))
All inputs are finite; a program needn't handle non-finite values.
Results may differ from a plain program's by a relative error of at most 0.04.
The roundings to bfloat16 on the way count: a program that leaves them out, or rounds other values in their place, can miss the bound.
Values may be sent and summed in bfloat16 or wider, within the bound.
A program may use at most 64 MiB of HBM per device.

v0:
```python
import functools
import math

import jax
import jax.numpy as jnp
from jax import lax
from jax.experimental import pallas as pl
from jax.experimental.pallas import tpu as pltpu
from jax.sharding import PartitionSpec as P

HD = 128
G = 6
MESH = pl.DeviceIdType.MESH

theta_base = 1000000.0
eps_norm = 1e-06
masked_score = -1e30

WQ, WKV, WO, KV, WQ_TAIL, WO_TAIL = range(6)
UP, DOWN, ACROSS, CORE = range(4)


def block_width(rows, limit):
    width = min(rows, limit)
    while rows % width:
        width -= 1
    return width


def kernel(
    sizes,
    tokens_ref,
    gain_ref,
    w_query_ref,
    w_key_ref,
    w_value_ref,
    q_bias_ref,
    k_bias_ref,
    v_bias_ref,
    w_out_ref,
    cos_ref,
    sin_ref,
    out_ref,
    wq,
    wkv,
    wo,
    kv,
    normed,
    query,
    attended,
    partial,
    outgoing,
    incoming,
    local_sem,
    send_sem,
    recv_sem,
    norm_send,
    norm_recv,
    sum_send,
    sum_recv,
):
    blocks, heads = sizes
    nz = blocks // 4
    me = lax.axis_index("blk")
    head = lax.axis_index("head")
    z, y, c = me // 4, (me // 2) % 2, me % 2
    local_rows, width = tokens_ref.shape
    group_rows = local_rows * heads
    heads_here = wq.shape[1] // HD
    kv_here = wkv.shape[1] // (2 * HD)
    per_kv = heads_here // kv_here
    kv_cols = kv_here * HD
    kv_start = pl.multiple_of((head * heads_here // G) * HD, HD)
    buffers = {WQ: wq, WKV: wkv, WO: wo, KV: kv, WQ_TAIL: wq, WO_TAIL: wo}
    queries, outs = (WQ, WQ_TAIL), (WO, WO_TAIL)
    scale = 1.0 / math.sqrt(HD)

    def slot_of(zz, yy, cc):
        return (zz * 2 + yy) * 2 + cc

    def rows_of(item, slot):
        each = buffers[item].shape[0] // blocks
        first, size = 0, each
        if item in queries + outs:
            cut = each // 2 // 16 * 16
            first, size = (0, cut) if item in (WQ, WO) else (cut, each - cut)
        return buffers[item].at[pl.ds(pl.multiple_of(slot * each + first, 16), size)]

    def whole_rows(ref):
        each = ref.shape[0] // blocks
        return ref.at[pl.ds(pl.multiple_of(me * each, each), each)]

    def target(route):
        step = {UP: 4, DOWN: -4, ACROSS: 2 - 4 * y, CORE: 1 - 2 * c}[route]
        return (me + step, head)

    def copy(item, slot, route):
        part = rows_of(item, slot)
        return pltpu.make_async_remote_copy(
            src_ref=part,
            dst_ref=part,
            send_sem=send_sem.at[item, slot, route],
            recv_sem=recv_sem.at[item, slot],
            device_id=target(route),
            device_id_type=MESH,
        )

    def send(item, slot, route):
        if route == UP:
            pl.when(z < nz - 1)(lambda: copy(item, slot, route).start())
        elif route == DOWN:
            pl.when(z > 0)(lambda: copy(item, slot, route).start())
        else:
            copy(item, slot, route).start()

    def sent(item, slot, route):
        if route == UP:
            pl.when(z < nz - 1)(lambda: copy(item, slot, route).wait_send())
        elif route == DOWN:
            pl.when(z > 0)(lambda: copy(item, slot, route).wait_send())
        else:
            copy(item, slot, route).wait_send()

    def arrived(item, slot):
        copy(item, slot, CORE).wait_recv()

    def below(k, act):
        pl.when(z >= k)(lambda: act(z - k))

    def above(k, act):
        pl.when(z + k < nz)(lambda: act(z + k))

    def z_step(item, k, yy, then=()):
        def from_below(zz):
            slot = slot_of(zz, yy, c)
            arrived(item, slot)
            for route in (UP,) + then:
                send(item, slot, route)

        def from_above(zz):
            slot = slot_of(zz, yy, c)
            arrived(item, slot)
            for route in (DOWN,) + then:
                send(item, slot, route)

        below(k, from_below)
        above(k, from_above)

    def at_distance(k, act):
        if k == 0:
            act(z)
        else:
            below(k, act)
            above(k, act)

    def across(item, k):
        def act(zz):
            slot = slot_of(zz, 1 - y, c)
            arrived(item, slot)
            send(item, slot, CORE)

        at_distance(k, act)

    def finish(item):
        for zz in range(nz):
            for yy in range(2):
                arrived(item, slot_of(zz, yy, 1 - c))

    def drain(item, both):
        for yy in (y, 1 - y) if both else (y,):
            for route in (UP, DOWN):
                sent(item, slot_of(z, yy, c), route)
            for k in range(1, nz):
                below(k, lambda zz, yy=yy: sent(item, slot_of(zz, yy, c), UP))
                above(k, lambda zz, yy=yy: sent(item, slot_of(zz, yy, c), DOWN))
        if both:
            sent(item, me, ACROSS)
        for zz in range(nz):
            if not both:
                sent(item, slot_of(zz, y, c), ACROSS)
            for yy in range(2):
                sent(item, slot_of(zz, yy, c), CORE)

    own = [
        pltpu.make_async_copy(w_query_ref, whole_rows(wq), local_sem.at[0]),
        pltpu.make_async_copy(
            w_key_ref.at[:, pl.ds(kv_start, kv_cols)],
            rows_of(WKV, me).at[:, pl.ds(0, kv_cols)],
            local_sem.at[1],
        ),
        pltpu.make_async_copy(
            w_value_ref.at[:, pl.ds(kv_start, kv_cols)],
            rows_of(WKV, me).at[:, pl.ds(kv_cols, kv_cols)],
            local_sem.at[2],
        ),
        pltpu.make_async_copy(w_out_ref, whole_rows(wo), local_sem.at[3]),
    ]
    for one in own:
        one.start()

    barrier = pltpu.get_barrier_semaphore()

    def greet(blk, hd):
        pl.semaphore_signal(barrier, inc=1, device_id=(blk, hd), device_id_type=MESH)

    pl.when(z < nz - 1)(lambda: greet(me + 4, head))
    pl.when(z > 0)(lambda: greet(me - 4, head))
    greet(target(ACROSS)[0], head)
    greet(target(CORE)[0], head)
    peers = [lax.rem(head + d, heads) for d in range(1, heads)]
    for peer in peers:
        greet(me, peer)
    ends = jnp.where(z < nz - 1, 1, 0) + jnp.where(z > 0, 1, 0)
    pl.semaphore_wait(barrier, ends + 2 + len(peers))

    own[1].wait()
    own[2].wait()
    for route in (ACROSS, UP, DOWN, CORE):
        send(WKV, me, route)
    own[0].wait()
    own[3].wait()
    for item in queries + outs:
        for route in (ACROSS, CORE):
            send(item, me, route)

    my_rows = pl.ds(pl.multiple_of(head * local_rows, local_rows), local_rows)
    floats = tokens_ref[...].astype(jnp.float32)
    normed[my_rows, :] = (
        floats
        * lax.rsqrt(jnp.mean(floats * floats, axis=1, keepdims=True) + eps_norm)
        * gain_ref[...]
    ).astype(jnp.bfloat16)

    there = slot_of(z, 1 - y, c)
    arrived(WKV, there)
    for route in (UP, DOWN, CORE):
        send(WKV, there, route)

    def norm_copy(d):
        return pltpu.make_async_remote_copy(
            src_ref=normed.at[my_rows],
            dst_ref=normed.at[my_rows],
            send_sem=norm_send.at[d],
            recv_sem=norm_recv.at[d],
            device_id=(me, peers[d]),
            device_id_type=MESH,
        )

    for d in range(len(peers)):
        norm_copy(d).start()

    for k in range(1, nz):
        z_step(WKV, k, y, (CORE,))
        z_step(WKV, k, 1 - y, (CORE,))
        if k == max(1, nz - 2):
            for item in queries:
                for route in (UP, DOWN):
                    send(item, me, route)
    for d in range(len(peers)):
        norm_copy(d).wait_recv()
    finish(WKV)

    cosine, sine = cos_ref[...], sin_ref[...]

    def turn(values):
        return values * cosine + pltpu.roll(values, HD // 2, 1) * sine

    kv_rows = pl.ds(pl.multiple_of(me * group_rows, group_rows), group_rows)
    sums = jnp.dot(normed[...], wkv[...], preferred_element_type=jnp.float32)
    for g in range(kv_here):
        bias = k_bias_ref[:, pl.ds(pl.multiple_of(kv_start + g * HD, HD), HD)]
        kv[kv_rows, pl.ds(g * HD, HD)] = turn(sums[:, g * HD : (g + 1) * HD] + bias).astype(
            jnp.bfloat16
        )
        bias = v_bias_ref[:, pl.ds(pl.multiple_of(kv_start + g * HD, HD), HD)]
        at = kv_cols + g * HD
        kv[kv_rows, pl.ds(at, HD)] = (sums[:, at : at + HD] + bias).astype(jnp.bfloat16)

    for item in queries:
        across(item, 0)
    for route in (UP, DOWN, ACROSS, CORE):
        send(KV, me, route)

    for k in range(1, nz):
        for item in queries:
            z_step(item, k, y, (ACROSS, CORE))
        z_step(KV, k, y, (ACROSS, CORE))
        if k == max(1, nz - 2):
            for item in outs:
                for route in (UP, DOWN):
                    send(item, me, route)
    for k in range(1, nz):
        if k == nz - 1:
            for item in outs:
                z_step(item, 1, y, (ACROSS, CORE))
        for item in queries:
            across(item, k)
    for k in range(nz):
        across(KV, k)
    for item in queries + (KV,):
        finish(item)

    joined = 2 if heads_here % 2 == 0 else 1

    def project(n, carry):
        cols = pl.ds(pl.multiple_of(n * joined * HD, joined * HD), joined * HD)
        total = jnp.dot(normed[...], wq[:, cols], preferred_element_type=jnp.float32)
        total = total + q_bias_ref[:, cols]
        for j in range(joined):
            query[n * joined + j] = turn(total[:, j * HD : (j + 1) * HD]).astype(jnp.bfloat16)
        return carry

    lax.fori_loop(0, heads_here // joined, project, 0)

    if nz > 2:
        for item in outs:
            z_step(item, 2, y, (ACROSS, CORE))

    keys = kv.shape[0]
    span = block_width(keys, 512)
    stacked = per_kv * group_rows
    last_query = me * group_rows + group_rows - 1
    steps = last_query // span + 1

    for g in range(kv_here):
        q = query[g * per_kv : (g + 1) * per_kv].reshape(stacked, HD)

        def attend(j, state, q=q, g=g):
            top, total, acc = state
            at = pl.ds(pl.multiple_of(j * span, span), span)
            scores = (
                lax.dot_general(
                    q,
                    kv[at, pl.ds(g * HD, HD)],
                    (((1,), (1,)), ((), ())),
                    preferred_element_type=jnp.float32,
                )
                * scale
            )
            shape = (per_kv, group_rows, span)
            rows = lax.broadcasted_iota(jnp.int32, shape, 1).reshape(stacked, span)
            columns = lax.broadcasted_iota(jnp.int32, (stacked, span), 1)
            visible = columns + j * span <= rows + me * group_rows
            scores = jnp.where(visible, scores, masked_score)
            new_top = jnp.maximum(top, jnp.max(scores, axis=1, keepdims=True))
            weights = jnp.where(visible, jnp.exp(scores - new_top), 0.0)
            fade = jnp.exp(top - new_top)
            total = total * fade + jnp.sum(weights, axis=1, keepdims=True)
            acc = acc * fade + jnp.dot(
                weights.astype(jnp.bfloat16),
                kv[at, pl.ds(kv_cols + g * HD, HD)],
                preferred_element_type=jnp.float32,
            )
            return (new_top, total, acc)

        start = (
            jnp.full((stacked, 1), masked_score, jnp.float32),
            jnp.zeros((stacked, 1), jnp.float32),
            jnp.zeros((stacked, HD), jnp.float32),
        )
        top, total, acc = lax.fori_loop(0, steps, attend, start)
        result = (acc / total).astype(jnp.bfloat16)
        for r in range(per_kv):
            attended[:, pl.ds((g * per_kv + r) * HD, HD)] = result[
                r * group_rows : (r + 1) * group_rows
            ]
        for k in range(3, nz):
            if g == 0:
                z_step(WO, k, y, (ACROSS, CORE))
    for k in range(3, nz):
        z_step(WO_TAIL, k, y, (ACROSS, CORE))

    each = wo.shape[0] // blocks
    grouped = (4 * each) % HD == 0
    groups = nz if grouped else 1
    chunk = width // groups

    def sum_copy(d, i, start):
        rows = pl.ds(pl.multiple_of(peers[d] * local_rows, local_rows), local_rows)
        cols = pl.ds(pl.multiple_of(start, HD), chunk)
        return pltpu.make_async_remote_copy(
            src_ref=outgoing.at[rows, cols],
            dst_ref=incoming.at[d, :, cols],
            send_sem=sum_send.at[d, i],
            recv_sem=sum_recv.at[d, i],
            device_id=(me, peers[d]),
            device_id_type=MESH,
        )

    def produce(start, size):
        cols = pl.ds(pl.multiple_of(start, HD), size)
        result = lax.dot_general(
            attended[...],
            wo[cols, :],
            (((1,), (1,)), ((), ())),
            preferred_element_type=jnp.float32,
        )
        partial[:, cols] = result
        outgoing[:, cols] = result.astype(jnp.bfloat16)

    def place(i):
        way = 1 - 2 * (z // max(1, nz // 2)) if nz > 1 else 1
        return lax.rem(z + way * i + nz, nz)

    if grouped:

        def produce_group(i, carry):
            zz = place(i)
            slot = slot_of(zz, 1 - y, c)
            for item in outs:
                arrived(item, slot)
                send(item, slot, CORE)
            for item in outs:
                for yy in range(2):
                    arrived(item, slot_of(zz, yy, 1 - c))
            produce(zz * 4 * each, chunk)
            for d in range(len(peers)):
                sum_copy(d, i, zz * chunk).start()
            return carry

        lax.fori_loop(0, nz, produce_group, 0)
    else:
        for item in outs:
            for k in range(nz):
                across(item, k)
            finish(item)
        part = 256
        lax.fori_loop(0, width // part, lambda n, carry: (produce(n * part, part), carry)[1], 0)
        for d in range(len(peers)):
            sum_copy(d, 0, 0).start()

    for item in queries + outs + (WKV, KV):
        drain(item, item == WKV)
    for d in range(len(peers)):
        norm_copy(d).wait_send()

    def collect(i, carry):
        start = place(i) * chunk if grouped else 0
        cols = pl.ds(pl.multiple_of(start, HD), chunk)
        for d in range(len(peers)):
            sum_copy(d, i, start).wait_recv()
        result = partial[my_rows, cols]
        for d in range(len(peers)):
            result = result + incoming[d, :, cols].astype(jnp.float32)
        out_ref[:, cols] = result.astype(jnp.bfloat16)
        for d in range(len(peers)):
            sum_copy(d, i, start).wait_send()
        return carry

    lax.fori_loop(0, groups, collect, 0)


def on_device(tokens, norm_gain, w_query, w_key, w_value, q_bias, k_bias, v_bias, w_out):
    blocks, heads = lax.axis_size("blk"), lax.axis_size("head")
    local_rows, width = tokens.shape
    group_rows = local_rows * heads
    heads_here = w_query.shape[1] // HD
    kv_here = max(1, heads_here // G)
    positions = lax.axis_index("blk") * group_rows + jnp.arange(group_rows, dtype=jnp.int32)
    half = HD // 2
    freq = theta_base ** (-(jnp.arange(half, dtype=jnp.float32) * 2.0 / HD))
    angles = positions.astype(jnp.float32)[:, None] * freq[None, :]
    cosine, sine = jnp.cos(angles), jnp.sin(angles)
    cosine = jnp.concatenate([cosine, cosine], axis=1)
    sine = jnp.concatenate([-sine, sine], axis=1)
    inner = heads_here * HD
    vmem = pl.BlockSpec(memory_space=pltpu.VMEM)
    hbm = pl.BlockSpec(memory_space=pl.ANY)
    others = max(1, heads - 1)
    bf16, f32 = jnp.bfloat16, jnp.float32
    return pl.pallas_call(
        functools.partial(kernel, (blocks, heads)),
        out_shape=jax.ShapeDtypeStruct((local_rows, width), bf16),
        in_specs=[vmem, vmem, hbm, hbm, hbm, vmem, vmem, vmem, hbm, vmem, vmem],
        out_specs=vmem,
        scratch_shapes=[
            pltpu.VMEM((width, inner), bf16),
            pltpu.VMEM((width, 2 * kv_here * HD), bf16),
            pltpu.VMEM((width, inner), bf16),
            pltpu.VMEM((blocks * group_rows, 2 * kv_here * HD), bf16),
            pltpu.VMEM((group_rows, width), bf16),
            pltpu.VMEM((heads_here, group_rows, HD), bf16),
            pltpu.VMEM((group_rows, inner), bf16),
            pltpu.VMEM((group_rows, width), f32),
            pltpu.VMEM((group_rows, width), bf16),
            pltpu.VMEM((others, local_rows, width), bf16),
            pltpu.SemaphoreType.DMA((4,)),
            pltpu.SemaphoreType.DMA((6, blocks, 4)),
            pltpu.SemaphoreType.DMA((6, blocks)),
            pltpu.SemaphoreType.DMA((others,)),
            pltpu.SemaphoreType.DMA((others,)),
            pltpu.SemaphoreType.DMA((others, blocks // 4)),
            pltpu.SemaphoreType.DMA((others, blocks // 4)),
        ],
        compiler_params=pltpu.CompilerParams(
            collective_id=0, has_side_effects=True, vmem_limit_bytes=60 * 1024 * 1024
        ),
    )(
        tokens,
        norm_gain[None, :],
        w_query,
        w_key,
        w_value,
        q_bias[None, :],
        k_bias[None, :],
        v_bias[None, :],
        w_out.T,
        cosine,
        sine,
    )


def solution(mesh):
    placed = (
        P(("blk", "head"), None),
        P(),
        P("blk", "head"),
        P("blk", None),
        P("blk", None),
        P("head"),
        P(),
        P(),
        P("head", "blk"),
    )
    return jax.shard_map(
        on_device, mesh=mesh, in_specs=placed, out_specs=P(("blk", "head"), None), check_vma=False
    )
```

profile of v0, /device:TPU:0, one launch (start us, length us, event | category | flops | bytes accessed | tf_op | source)
XLA Modules:
  0.0 161.0 jit_solution(15214871503936972167)
XLA Ops:
  0.0 0.0 copy-start.1
  0.0 0.0 copy-start
  0.0 0.7 copy-done.1
  0.7 0.6 broadcast_in_dim.15.q_bias_ref
  1.3 0.0 copy-done
  1.3 0.6 broadcast_in_dim.14.gain_ref
  1.9 0.3 fusion
  2.2 0.7 pad_maximum_fusion
  3.0 156.2 %shard_map.91 = bf16[64,3584]{1,0:T(8,128)(2,1)} custom-call(bf16[64,3584]{1,0:T(8,128)(2,1)} %tokens_ref.1, f32[1,3584]{1,0:T(1,128)} %broadcast_in_dim.14.gain_ref, bf16[224,1536]{1,0:T(8,128)(2,1)} %w_query_ref.1, bf16[224,512]{1,0:T(8,128)(2,1)} %w_key_ref.1, bf16[224,512]{1,0:T(8,128)(2,1)} %w_value_ref.1, f32[1,1536]{1,0:T(1,128)} %broadcast_in_dim.15.q_bias_ref, ...), custom_call_target="tpu_custom_call" | custom-call | tf_op jit(solution)/shard_map/pallas_call | solution.py:471
  159.2 1.8 %copy.11 = bf16[64,3584]{1,0:T(8,128)(2,1)} copy(bf16[64,3584]{1,0:T(8,128)(2,1)} %shard_map.91) | data formatting | bytes 917504
  (2 shorter events, 0.0 us)
Async XLA Ops:
  0.0 0.7 copy-start.1
  0.0 1.3 copy-start
where the time goes:
time: 161 us
  Pallas kernels  156 us (97%)
  local copies, waits for them, and re-layouts  3.7 us (2%)
    pallas_call x1, Pallas kernels, on_device(): pl.pallas_call(functools.partial(kernel, (blocks, heads)), out_shape=jax....  156 us

commit v1 on v0

--- a/solution.py
+++ b/solution.py
@@ -510,6 +510,557 @@
     )
 
 
+def plane_kernel(
+    nz,
+    tokens_ref,
+    gain_ref,
+    w_query_ref,
+    w_key_ref,
+    w_value_ref,
+    q_bias_ref,
+    k_bias_ref,
+    v_bias_ref,
+    w_out_ref,
+    cos_ref,
+    sin_ref,
+    out_ref,
+    stage,
+    w,
+    normed,
+    xs,
+    part_out,
+    part_in,
+    own,
+    biases,
+    kv,
+    hidden,
+    att,
+    att_other,
+    wo,
+    acc,
+    outs,
+    result,
+    load_sem,
+    wo_load_sem,
+    first_send,
+    w_send,
+    w_recv,
+    x_send,
+    x_recv,
+    b_send,
+    b_recv,
+    p_send,
+    p_recv,
+    kv_send,
+    kv_recv,
+    a_send,
+    a_recv,
+    wo_send,
+    wo_recv,
+    o_send,
+    o_recv,
+):
+    f32, bf16 = jnp.float32, jnp.bfloat16
+    me = lax.axis_index("blk")
+    x = lax.axis_index("head")
+    z, y, c = me // 4, (me // 2) % 2, me % 2
+    rows, width = tokens_ref.shape
+    each = w_query_ref.shape[0]
+    depth = width // 2
+    per_core = G // 2
+    chunks = per_core + 1
+    columns = width // nz
+    zh, par = z // 2, ((z + 1) // 2) % 2
+    pair, mirror = z + 1 - 2 * (z % 2), nz - 1 - z
+    group = 2 * zh + par
+    waiting = []
+
+    def dev(zz, yy, cc, xx):
+        return ((zz * 2 + yy) * 2 + cc, xx)
+
+    core_peer = dev(z, y, 1 - c, x)
+    x_peer = dev(z, y, c, 1 - x)
+    y_peer = dev(z, 1 - y, c, x)
+    diagonal = dev(z, 1 - y, c, 1 - x)
+
+    def remote(src, dst, ssem, rsem, to):
+        return pltpu.make_async_remote_copy(
+            src_ref=src, dst_ref=dst, send_sem=ssem, recv_sem=rsem, device_id=to, device_id_type=MESH
+        )
+
+    def go(src, dst, ssem, rsem, to, when=None):
+        one = remote(src, dst, ssem, rsem, to)
+        if when is None:
+            one.start()
+            waiting.append(one.wait_send)
+        else:
+            pl.when(when)(one.start)
+            waiting.append(lambda: pl.when(when)(one.wait_send))
+
+    def got(dst, rsem, when=None):
+        one = remote(dst, dst, b_send.at[0], rsem, x_peer)
+        if when is None:
+            one.wait_recv()
+        else:
+            pl.when(when)(one.wait_recv)
+
+    def slot(zs, yy, cc):
+        return (zs * 2 + yy) * 2 + cc
+
+    zs = z % 2
+    mine = slot(zs, y, c)
+
+    def block(xx, j, rb):
+        return w.at[xx, j, pl.ds(pl.multiple_of(rb * each, 16), each)]
+
+    def source(e, f, j):
+        p, cc = (par + e) % 2, (c + f) % 2
+        if j == 0:
+            at = pl.ds(pl.multiple_of((2 * x + p) * HD, HD), HD)
+            return cc, w_key_ref.at[:, at], w_value_ref.at[:, at]
+        at = pl.ds(pl.multiple_of((p * G + cc * per_core + j - 1) * HD, HD), HD)
+        return None, w_query_ref.at[:, at], None
+
+    def place(e, f, j):
+        return block(x, j, mine) if (e, f) == (0, 0) else stage.at[e, f, j]
+
+    def load(e, f, j):
+        cc, first, second = source(e, f, j)
+        sem = load_sem.at[e, f, j]
+        if second is None:
+            pltpu.make_async_copy(first, place(e, f, j), sem).start()
+        else:
+            pl.when(cc == 0)(pltpu.make_async_copy(first, place(e, f, j), sem).start)
+            pl.when(cc == 1)(pltpu.make_async_copy(second, place(e, f, j), sem).start)
+
+    def loaded(e, f, j):
+        pltpu.make_async_copy(source(e, f, j)[1], place(e, f, j), load_sem.at[e, f, j]).wait()
+
+    for j in range(chunks):
+        for e in range(2):
+            for f in range(2):
+                load(e, f, j)
+
+    barrier = pltpu.get_barrier_semaphore()
+    friends = [core_peer, x_peer, y_peer, diagonal]
+    for d in range(1, nz):
+        for f in range(2):
+            friends.append(dev((z + d) % nz, y, (c + f) % 2, x))
+    for friend in friends:
+        pl.semaphore_signal(barrier, inc=1, device_id=friend, device_id_type=MESH)
+    pl.semaphore_wait(barrier, len(friends))
+
+    def spread(xx, j, rb, to_x, to_y):
+        if to_x:
+            go(block(xx, j, rb), block(xx, j, rb), w_send.at[xx, j, rb, 0], w_recv.at[xx, j, rb], x_peer)
+        if to_y:
+            go(block(xx, j, rb), block(xx, j, rb), w_send.at[xx, j, rb, 1], w_recv.at[xx, j, rb], y_peer)
+
+    def arrived(xx, j, rb):
+        got(block(xx, j, rb), w_recv.at[xx, j, rb])
+
+    def begin(j):
+        loaded(0, 0, j)
+        spread(x, j, mine, True, True)
+        for f in range(2):
+            loaded(1, f, j)
+            go(
+                stage.at[1, f, j],
+                block(x, j, mine),
+                first_send.at[1, f, j],
+                w_recv.at[x, j, mine],
+                dev(pair, y, (c + f) % 2, x),
+            )
+        loaded(0, 1, j)
+        go(stage.at[0, 1, j], block(x, j, mine), first_send.at[0, 1, j], w_recv.at[x, j, mine], core_peer)
+
+    def home(j):
+        for rb in (slot(zs, y, 1 - c), slot(1 - zs, y, c), slot(1 - zs, y, 1 - c)):
+            arrived(x, j, rb)
+            spread(x, j, rb, True, True)
+
+    def relay_weights(j):
+        for zz in (zs, 1 - zs):
+            rb = slot(zz, 1 - y, 0)
+            arrived(x, j, rb)
+            spread(x, j, rb, True, False)
+            rb = slot(zz, y, 1)
+            arrived(1 - x, j, rb)
+            spread(1 - x, j, rb, False, True)
+
+    def rest_of_weights(j):
+        for zz in (zs, 1 - zs):
+            arrived(x, j, slot(zz, 1 - y, 1))
+            arrived(1 - x, j, slot(zz, y, 0))
+            for cc in range(2):
+                arrived(1 - x, j, slot(zz, 1 - y, cc))
+
+    begin(0)
+
+    floats = tokens_ref[...].astype(f32)
+    values = (
+        floats
+        * lax.rsqrt(jnp.mean(floats * floats, axis=1, keepdims=True) + eps_norm)
+        * gain_ref[...]
+    ).astype(bf16)
+    normed[0] = values[:, :depth]
+    normed[1] = values[:, depth:]
+
+    def token_rows(zz, cc):
+        return xs.at[pl.ds(pl.multiple_of((zz * 2 + cc) * rows, rows), rows)]
+
+    at_me = pl.ds(pl.multiple_of((z * 2 + c) * rows, rows), rows)
+    xs[at_me, :] = jnp.where(zh == 0, values[:, :depth], values[:, depth:])
+    biases[x] = q_bias_ref[...]
+
+    near, far = 2 - zh, 3 - 3 * zh
+    go(normed.at[zh], token_rows(z, c), x_send.at[0], x_recv.at[z * 2 + c], dev(pair, y, c, x))
+    go(normed.at[1 - zh], token_rows(z, c), x_send.at[1], x_recv.at[z * 2 + c], dev(near, y, c, x))
+    go(normed.at[zh], token_rows(z, c), x_send.at[2], x_recv.at[z * 2 + c], core_peer)
+    go(biases.at[x], biases.at[x], b_send.at[0], b_recv.at[0], x_peer)
+
+    begin(1)
+    home(0)
+
+    def pass_tokens(zz, n):
+        got(token_rows(zz, c), x_recv.at[zz * 2 + c])
+        if n:
+            go(
+                token_rows(zz, c),
+                token_rows(zz, c),
+                x_send.at[2 + n],
+                x_recv.at[zz * 2 + c],
+                dev(pair, y, c, x),
+                par == 1,
+            )
+        go(token_rows(zz, c), token_rows(zz, c), x_send.at[5 + n], x_recv.at[zz * 2 + c], core_peer)
+
+    pass_tokens(pair, 0)
+    relay_weights(0)
+    home(1)
+    pass_tokens(near, 1)
+    pass_tokens(far, 2)
+    begin(2)
+    begin(3)
+
+    wo_cols = 2 * 2 * HD
+    half_rows = each // 2
+
+    def wo_block(h, xx, s, half):
+        first = pl.multiple_of(s * each + half * half_rows, 16)
+        return wo.at[h, pl.ds(first, half_rows), pl.ds(pl.multiple_of(xx * wo_cols, HD), wo_cols)]
+
+    wo_loads = []
+    for h in range(per_core):
+        for gl in range(2):
+            for cc in range(2):
+                zz = x * (3 - gl) + (1 - x) * gl
+                wo_loads.append(
+                    pltpu.make_async_copy(
+                        w_out_ref.at[:, pl.ds((gl * G + cc * per_core + h) * HD, HD)],
+                        wo.at[
+                            h,
+                            pl.ds(pl.multiple_of((y * 2 + c) * each, 16), each),
+                            pl.ds(pl.multiple_of((zz * 2 + cc) * HD, HD), HD),
+                        ],
+                        wo_load_sem.at[h, gl, cc],
+                    )
+                )
+                wo_loads[-1].start()
+
+    for zz in range(1, nz + 1):
+        at = (z + zz) % nz
+        got(token_rows(at, 1 - c), x_recv.at[at * 2 + 1 - c])
+
+    def multiply(j):
+        rest_of_weights(j)
+        theirs = jnp.dot(xs[...], w[1 - zh, j], preferred_element_type=f32)
+        part_out[j] = theirs.astype(bf16)
+        go(part_out.at[j], part_in.at[j], p_send.at[j], p_recv.at[j], dev(mirror, y, c, x))
+        own[j] = jnp.dot(xs[...], w[zh, j], preferred_element_type=f32)
+
+    multiply(0)
+    relay_weights(1)
+    home(2)
+    multiply(1)
+    relay_weights(2)
+    home(3)
+
+    def turn(values):
+        return values * cos_ref[...] + pltpu.roll(values, HD // 2, 1) * sin_ref[...]
+
+    src = y * 2 + x
+    at_group = pl.ds(pl.multiple_of(group * HD, HD), HD)
+    got(part_in.at[0], p_recv.at[0])
+    total = own[0] + part_in[0].astype(f32)
+    kv[c, src] = jnp.where(
+        c == 0, turn(total + k_bias_ref[:, at_group]), total + v_bias_ref[:, at_group]
+    ).astype(bf16)
+
+    def kv_go(kind, s, n, to):
+        go(kv.at[kind, s], kv.at[kind, s], kv_send.at[n], kv_recv.at[kind, s], to)
+
+    def kv_got(kind, s):
+        got(kv.at[kind, s], kv_recv.at[kind, s])
+
+    kv_go(c, src, 0, x_peer)
+    kv_go(c, src, 1, y_peer)
+    kv_go(c, src, 2, diagonal)
+    kv_go(c, src, 3, core_peer)
+
+    multiply(2)
+    relay_weights(3)
+
+    at = jax.lax.broadcasted_iota(jnp.int32, (2 * rows, 8 * rows), 1)
+    within = at % (2 * rows)
+    key_at = (
+        (at // (4 * rows)) * 4 + (within // rows) * 2 + (at // (2 * rows)) % 2
+    ) * rows + within % rows
+    at = jax.lax.broadcasted_iota(jnp.int32, (2 * rows, 8 * rows), 0)
+    query_at = (y * 4 + (at // rows) * 2 + x) * rows + at % rows
+    hidden[...] = jnp.where(key_at <= query_at, 0.0, masked_score)
+
+    others = [(1 - y) * 2 + x, y * 2 + 1 - x, (1 - y) * 2 + 1 - x]
+    for n, s in enumerate(others):
+        kv_got(c, s)
+        kv_go(c, s, 4 + n, core_peer)
+    got(biases.at[1 - x], b_recv.at[0])
+    for s in [src] + others:
+        kv_got(1 - c, s)
+
+    factor = math.log2(math.e) / math.sqrt(HD)
+    cols_of_me = pl.ds(pl.multiple_of((z * 2 + c) * HD, HD), HD)
+
+    def att_piece(h, zz, cc):
+        return att.at[h, :, pl.ds(pl.multiple_of((zz * 2 + cc) * HD, HD), HD)]
+
+    def attend(h):
+        got(part_in.at[h + 1], p_recv.at[h + 1])
+        at = pl.ds(pl.multiple_of((par * G + c * per_core + h) * HD, HD), HD)
+        total = own[h + 1] + part_in[h + 1].astype(f32) + biases[zh, :, at]
+        query = turn(total).astype(bf16)
+        for t in range(nz):
+            q = query[t * 2 * rows : (t + 1) * 2 * rows]
+            scores = []
+            for u in range(t + 1):
+                keys = kv[0, :, u * 2 * rows : (u + 1) * 2 * rows].reshape(8 * rows, HD)
+                one = lax.dot_general(
+                    q, keys, (((1,), (1,)), ((), ())), preferred_element_type=f32
+                )
+                scores.append(one + hidden[...] if u == t else one)
+            top = jnp.max(functools.reduce(jnp.maximum, scores), axis=1, keepdims=True)
+            mixed, sums = None, None
+            for u in range(t + 1):
+                weights = jnp.exp2((scores[u] - top) * factor)
+                sums = weights if sums is None else sums + weights
+                vals = kv[1, :, u * 2 * rows : (u + 1) * 2 * rows].reshape(8 * rows, HD)
+                one = jnp.dot(weights.astype(bf16), vals, preferred_element_type=f32)
+                mixed = one if mixed is None else mixed + one
+            mixed = (mixed / jnp.sum(sums, axis=1, keepdims=True)).astype(bf16)
+            low, high = mixed[:rows], mixed[rows:]
+            att[h, t * rows : (t + 1) * rows, cols_of_me] = jnp.where(c == 0, low, high)
+            att_other[h, t * rows : (t + 1) * rows, :] = jnp.where(c == 0, high, low)
+        index = z * 2 + c
+        for way, ok in ((1, z < nz - 1), (-1, z > 0)):
+            n = 0 if way == 1 else 1
+            go(att_piece(h, z, c), att_piece(h, z, c), a_send.at[h, index, n], a_recv.at[h, index], dev(z + way, y, c, x), ok)
+            go(att_other.at[h], att_piece(h, z, c), a_send.at[h, index, 2 + n], a_recv.at[h, index], dev(z + way, y, 1 - c, x), ok)
+        go(att_other.at[h], att_piece(h, z, c), a_send.at[h, index, 4], a_recv.at[h, index], core_peer)
+
+    def relay_attended(h, k):
+        for way, here, more in ((1, z - k >= 0, z < nz - 1), (-1, z + k < nz, z > 0)):
+            zz = z - way * k
+            for cc in range(2):
+                def act(zz=zz, cc=cc):
+                    got(att_piece(h, zz, cc), a_recv.at[h, zz * 2 + cc])
+
+                pl.when(here)(act)
+                if k < nz - 1:
+                    go(
+                        att_piece(h, zz, cc),
+                        att_piece(h, zz, cc),
+                        a_send.at[h, zz * 2 + cc, 0 if way == 1 else 1],
+                        a_recv.at[h, zz * 2 + cc],
+                        dev(z + way, y, c, x),
+                        jnp.logical_and(here, more),
+                    )
+
+    def wo_go(h, xx, s, half, n, to):
+        go(wo_block(h, xx, s, half), wo_block(h, xx, s, half), wo_send.at[h, xx, s, half, n], wo_recv.at[h, xx, s, half], to)
+
+    def wo_got(h, xx, s, half):
+        got(wo_block(h, xx, s, half), wo_recv.at[h, xx, s, half])
+
+    def wo_begin(h):
+        for one in wo_loads[4 * h : 4 * h + 4]:
+            one.wait()
+        for half in range(2):
+            for n, to in enumerate((x_peer, y_peer, core_peer)):
+                wo_go(h, x, y * 2 + c, half, n, to)
+
+    def wo_relay(h):
+        for half in (0, 1):
+            wo_got(h, x, (1 - y) * 2 + c, half)
+            if half == 0:
+                wo_go(h, x, (1 - y) * 2 + c, half, 0, x_peer)
+            wo_go(h, x, (1 - y) * 2 + c, half, 2, core_peer)
+            wo_got(h, 1 - x, y * 2 + c, half)
+            if half == 1:
+                wo_go(h, 1 - x, y * 2 + c, half, 1, y_peer)
+            wo_go(h, 1 - x, y * 2 + c, half, 2, core_peer)
+
+    def wo_finish(h):
+        for half in (0, 1):
+            wo_got(h, 1 - x, (1 - y) * 2 + c, half)
+            wo_go(h, 1 - x, (1 - y) * 2 + c, half, 2, core_peer)
+        for half in (0, 1):
+            for xx in (x, 1 - x):
+                for yy in (y, 1 - y):
+                    wo_got(h, xx, yy * 2 + 1 - c, half)
+
+    def produce(h):
+        got(att_piece(h, z, 1 - c), a_recv.at[h, z * 2 + 1 - c])
+        for first in range(0, columns, 512):
+            size = min(512, columns - first)
+            part = lax.dot_general(
+                att[h], wo[h, first : first + size, :], (((1,), (1,)), ((), ())), preferred_element_type=f32
+            )
+            if h:
+                part = part + acc[:, first : first + size]
+            if h < per_core - 1:
+                acc[:, first : first + size] = part
+            else:
+                for t in range(nz):
+                    outs[t, :, first : first + size] = part[t * rows : (t + 1) * rows].astype(bf16)
+
+    wo_begin(0)
+    attend(0)
+    multiply(3)
+    wo_begin(1)
+    wo_relay(0)
+    relay_attended(0, 1)
+    attend(1)
+    wo_begin(2)
+    relay_attended(0, 2)
+    wo_relay(1)
+    relay_attended(1, 1)
+    attend(2)
+    relay_attended(0, 3)
+    wo_finish(0)
+    relay_attended(1, 2)
+    relay_attended(2, 1)
+    wo_relay(2)
+    produce(0)
+    relay_attended(2, 2)
+    relay_attended(1, 3)
+    wo_finish(1)
+    produce(1)
+    wo_finish(2)
+    relay_attended(2, 3)
+    produce(2)
+
+    def result_cols(zz):
+        return pl.ds(pl.multiple_of(zz * columns, HD), columns)
+
+    for d in range(1, nz):
+        go(outs.at[(z + d) % nz], result.at[:, result_cols(z)], o_send.at[d - 1], o_recv.at[z], dev((z + d) % nz, y, c, x))
+    out_ref[:, result_cols(z)] = outs[z]
+    for done in waiting:
+        done()
+    for d in range(1, nz):
+        zz = (z + d) % nz
+        got(result.at[:, result_cols(zz)], o_recv.at[zz])
+        out_ref[:, result_cols(zz)] = result[:, result_cols(zz)]
+
+
+def in_planes(tokens, norm_gain, w_query, w_key, w_value, q_bias, k_bias, v_bias, w_out):
+    blocks = lax.axis_size("blk")
+    nz = blocks // 4
+    rows, width = tokens.shape
+    me, x = lax.axis_index("blk"), lax.axis_index("head")
+    inner, each, per_core = w_query.shape[1], w_query.shape[0], G // 2
+    chunks, held, columns = per_core + 1, 2 * nz * rows, width // nz
+    where = jnp.arange(held, dtype=jnp.int32)
+    there = (where // (2 * rows)) * 4 + ((me // 2) % 2) * 2 + (where // rows) % 2
+    positions = (there * 2 + x) * rows + where % rows
+    half = HD // 2
+    freq = theta_base ** (-(jnp.arange(half, dtype=jnp.float32) * 2.0 / HD))
+    angles = positions.astype(jnp.float32)[:, None] * freq[None, :]
+    cosine, sine = jnp.cos(angles), jnp.sin(angles)
+    cosine = jnp.concatenate([cosine, cosine], axis=1)
+    sine = jnp.concatenate([-sine, sine], axis=1)
+    vmem = pl.BlockSpec(memory_space=pltpu.VMEM)
+    hbm = pl.BlockSpec(memory_space=pl.ANY)
+    bf16, f32 = jnp.bfloat16, jnp.float32
+    dma = pltpu.SemaphoreType.DMA
+    return pl.pallas_call(
+        functools.partial(plane_kernel, nz),
+        out_shape=jax.ShapeDtypeStruct((rows, width), bf16),
+        in_specs=[vmem, vmem, hbm, hbm, hbm, vmem, vmem, vmem, hbm, vmem, vmem],
+        out_specs=vmem,
+        scratch_shapes=[
+            pltpu.VMEM((2, 2, chunks, each, HD), bf16),
+            pltpu.VMEM((2, chunks, 8 * each, HD), bf16),
+            pltpu.VMEM((2, rows, width // 2), bf16),
+            pltpu.VMEM((held, width // 2), bf16),
+            pltpu.VMEM((chunks, held, HD), bf16),
+            pltpu.VMEM((chunks, held, HD), bf16),
+            pltpu.VMEM((chunks, held, HD), f32),
+            pltpu.VMEM((2, 1, inner), f32),
+            pltpu.VMEM((2, 4, held, HD), bf16),
+            pltpu.VMEM((2 * rows, 8 * rows), f32),
+            pltpu.VMEM((per_core, nz * rows, 2 * nz * HD), bf16),
+            pltpu.VMEM((per_core, nz * rows, HD), bf16),
+            pltpu.VMEM((per_core, columns, 2 * nz * HD), bf16),
+            pltpu.VMEM((nz * rows, columns), f32),
+            pltpu.VMEM((nz, rows, columns), bf16),
+            pltpu.VMEM((rows, width), bf16),
+            dma((2, 2, chunks)),
+            dma((per_core, 2, 2)),
+            dma((2, 2, chunks)),
+            dma((2, chunks, 8, 2)),
+            dma((2, chunks, 8)),
+            dma((8,)),
+            dma((2 * nz,)),
+            dma((1,)),
+            dma((1,)),
+            dma((chunks,)),
+            dma((chunks,)),
+            dma((7,)),
+            dma((2, 4)),
+            dma((per_core, 2 * nz, 5)),
+            dma((per_core, 2 * nz)),
+            dma((per_core, 2, 4, 2, 3)),
+            dma((per_core, 2, 4, 2)),
+            dma((nz - 1,)),
+            dma((nz,)),
+        ],
+        compiler_params=pltpu.CompilerParams(
+            collective_id=1, has_side_effects=True, vmem_limit_bytes=60 * 1024 * 1024
+        ),
+    )(
+        tokens,
+        norm_gain[None, :],
+        w_query,
+        w_key,
+        w_value,
+        q_bias[None, :],
+        k_bias[None, :],
+        v_bias[None, :],
+        w_out.T,
+        cosine,
+        sine,
+    )
+
+
+def by_mesh(tokens, norm_gain, w_query, w_key, *rest):
+    blocks, heads = lax.axis_size("blk"), lax.axis_size("head")
+    groups = w_key.shape[1] // HD
+    fits = blocks == 16 and heads == 2 and groups == 4 and w_query.shape[1] == 2 * G * HD
+    run = in_planes if fits else on_device
+    return run(tokens, norm_gain, w_query, w_key, *rest)
+
+
 def solution(mesh):
     placed = (
         P(("blk", "head"), None),
@@ -523,5 +1074,5 @@
         P("head", "blk"),
     )
     return jax.shard_map(
-        on_device, mesh=mesh, in_specs=placed, out_specs=P(("blk", "head"), None), check_vma=False
+        by_mesh, mesh=mesh, in_specs=placed, out_specs=P(("blk", "head"), None), check_vma=False
     )

time: 161 us -> 114 us (0.71)
  Pallas kernels: 156 us -> 108 us
    pallas_call x1, Pallas kernels: 156 us -> 108 us  [in_planes(): pl.pallas_call(functools.partial(plane_kernel, nz), out_shape=jax.ShapeDt...]
where the time goes in v1:
time: 114 us
  Pallas kernels  108 us (95%)
  local copies, waits for them, and re-layouts  3.12 us (3%)
  other arithmetic  2.01 us (2%)
    pallas_call x1, Pallas kernels, in_planes(): pl.pallas_call(functools.partial(plane_kernel, nz), out_shape=jax.ShapeDt...  108 us

profile of v1, /device:TPU:0, one launch (start us, length us, event | category | flops | bytes accessed | tf_op | source)
XLA Modules:
  0.0 113.5 jit_solution(5710422859517454477)
XLA Ops:
  0.0 1.0 fusion
  1.0 0.0 copy-start
  1.0 1.0 pad_maximum_fusion
  2.0 0.0 copy-done
  2.0 0.0 copy-start.1
  2.0 0.6 broadcast_in_dim.14.gain_ref
  2.6 0.1 copy-done.1
  2.7 0.6 broadcast_in_dim.15.q_bias_ref
  3.3 108.4 %shard_map.91 = bf16[64,3584]{1,0:T(8,128)(2,1)} custom-call(bf16[64,3584]{1,0:T(8,128)(2,1)} %tokens_ref.1, f32[1,3584]{1,0:T(1,128)} %broadcast_in_dim.14.gain_ref, bf16[224,1536]{1,0:T(8,128)(2,1)} %w_query_ref.1, bf16[224,512]{1,0:T(8,128)(2,1)} %w_key_ref.1, bf16[224,512]{1,0:T(8,128)(2,1)} %w_value_ref.1, f32[1,1536]{1,0:T(1,128)} %broadcast_in_dim.15.q_bias_ref, ...), custom_call_target="tpu_custom_call" | custom-call | tf_op jit(solution)/shard_map/pallas_call | solution.py:996
  111.7 1.8 %copy.11 = bf16[64,3584]{1,0:T(8,128)(2,1)} copy(bf16[64,3584]{1,0:T(8,128)(2,1)} %shard_map.91) | data formatting | bytes 917504
  (2 shorter events, 0.0 us)
Async XLA Ops:
  1.0 1.0 copy-start
  2.0 0.7 copy-start.1

commit v2 on v0

--- a/solution.py
+++ b/solution.py
@@ -510,6 +510,662 @@
     )
 
 
+def plane_kernel(
+    nz,
+    tokens_ref,
+    gain_ref,
+    w_query_ref,
+    w_key_ref,
+    w_value_ref,
+    q_bias_ref,
+    k_bias_ref,
+    v_bias_ref,
+    w_out_ref,
+    base_cos_ref,
+    base_sin_ref,
+    out_ref,
+    tokens,
+    gain,
+    q_flat,
+    k_bias,
+    v_bias,
+    cosine,
+    sine,
+    stage,
+    w,
+    normed,
+    xs,
+    part_out,
+    part_in,
+    full,
+    biases,
+    kv,
+    hidden,
+    att,
+    att_other,
+    wo,
+    acc,
+    outs,
+    result,
+    small_sem,
+    load_sem,
+    wo_load_sem,
+    w_send,
+    w_home,
+    w_relay,
+    w_rest,
+    x_send,
+    x_recv,
+    b_sem,
+    p_send,
+    p_recv,
+    kv_send,
+    kv_recv,
+    a_send,
+    a_recv,
+    wo_send,
+    wo_recv,
+    o_sem,
+):
+    f32, bf16 = jnp.float32, jnp.bfloat16
+    me = lax.axis_index("blk")
+    x = lax.axis_index("head")
+    z, y, c = me // 4, (me // 2) % 2, me % 2
+    rows, width = tokens_ref.shape
+    each = w_query_ref.shape[0]
+    depth = width // nz
+    per_core = G // 2
+    chunks = per_core + 1
+    columns = width // nz
+    zh = z // 2
+    inner = ((z + 1) // 2) % 2 == 1
+    outer = jnp.logical_not(inner)
+    pair = z + 1 - 2 * (z % 2)
+    near, far = 2 - zh, 3 - 3 * zh
+    final_waits = []
+
+    def dev(zz, yy, cc, xx):
+        return ((zz * 2 + yy) * 2 + cc, xx)
+
+    core_peer = dev(z, y, 1 - c, x)
+    x_peer = dev(z, y, c, 1 - x)
+    y_peer = dev(z, 1 - y, c, x)
+    diagonal = dev(z, 1 - y, c, 1 - x)
+
+    def go(src, dst, ssem, rsem, to, when=None):
+        one = pltpu.make_async_remote_copy(
+            src_ref=src, dst_ref=dst, send_sem=ssem, recv_sem=rsem, device_id=to, device_id_type=MESH
+        )
+        if when is None:
+            one.start()
+        else:
+            pl.when(when)(one.start)
+
+    def got(like, rsem):
+        pltpu.make_async_remote_copy(
+            src_ref=like, dst_ref=like, send_sem=b_sem.at[0], recv_sem=rsem, device_id=x_peer, device_id_type=MESH
+        ).wait_recv()
+
+    def at_end(like, ssem, when=None):
+        one = pltpu.make_async_remote_copy(
+            src_ref=like, dst_ref=like, send_sem=ssem, recv_sem=b_sem.at[1], device_id=x_peer, device_id_type=MESH
+        )
+        if when is None:
+            final_waits.append(one.wait_send)
+        else:
+            final_waits.append(lambda: pl.when(when)(one.wait_send))
+
+    small = [
+        pltpu.make_async_copy(tokens_ref, tokens, small_sem.at[0]),
+        pltpu.make_async_copy(gain_ref, gain, small_sem.at[1]),
+        pltpu.make_async_copy(q_bias_ref, q_flat, small_sem.at[2]),
+        pltpu.make_async_copy(k_bias_ref, k_bias, small_sem.at[3]),
+        pltpu.make_async_copy(v_bias_ref, v_bias, small_sem.at[4]),
+    ]
+    for one in small:
+        one.start()
+
+    barrier = pltpu.get_barrier_semaphore()
+    friends = [core_peer, x_peer, y_peer, diagonal]
+    for d in range(1, nz):
+        for f in range(2):
+            friends.append(dev((z + d) % nz, y, (c + f) % 2, x))
+    for friend in friends:
+        pl.semaphore_signal(barrier, inc=1, device_id=friend, device_id_type=MESH)
+
+    mine = y * 2 + c
+
+    def block(xx, j, s):
+        return w.at[
+            j,
+            pl.ds(pl.multiple_of(s * each, 16), each),
+            pl.ds(pl.multiple_of(xx * 2 * HD, HD), 2 * HD),
+        ]
+
+    def blocks_like(n):
+        return w.at[0, pl.ds(0, n * each), pl.ds(0, 2 * HD)]
+
+    def load(f, j):
+        place = stage.at[j] if f else block(x, j, mine)
+        cc = (c + f) % 2
+        sem = load_sem.at[j]
+        if j == 0:
+            at = pl.ds(pl.multiple_of(2 * x * HD, HD), 2 * HD)
+            pl.when(cc == 0)(pltpu.make_async_copy(w_key_ref.at[:, at], place, sem).start)
+            pl.when(cc == 1)(pltpu.make_async_copy(w_value_ref.at[:, at], place, sem).start)
+        else:
+            for gl in range(2):
+                at = pl.ds(pl.multiple_of((gl * G + cc * per_core + j - 1) * HD, HD), HD)
+                pltpu.make_async_copy(
+                    w_query_ref.at[:, at], place.at[:, pl.ds(gl * HD, HD)], sem
+                ).start()
+
+    def loaded(j):
+        pltpu.make_async_copy(blocks_like(2), blocks_like(2), load_sem.at[j]).wait()
+
+    for j in range(chunks):
+        for f in range(2):
+            load(f, j)
+
+    wo_cols = 2 * 2 * HD
+    half_rows = each // 2
+
+    def wo_block(h, xx, s, half):
+        first = pl.multiple_of(s * each + half * half_rows, 16)
+        return wo.at[h, pl.ds(first, half_rows), pl.ds(pl.multiple_of(xx * wo_cols, HD), wo_cols)]
+
+    def wo_like(n):
+        return wo.at[0, pl.ds(0, n * half_rows), pl.ds(0, wo_cols)]
+
+    for h in range(per_core):
+        for gl in range(2):
+            for cc in range(2):
+                zz = 2 * x + gl
+                pltpu.make_async_copy(
+                    w_out_ref.at[:, pl.ds((gl * G + cc * per_core + h) * HD, HD)],
+                    wo.at[
+                        h,
+                        pl.ds(pl.multiple_of((y * 2 + c) * each, 16), each),
+                        pl.ds(pl.multiple_of((zz * 2 + cc) * HD, HD), HD),
+                    ],
+                    wo_load_sem.at[h],
+                ).start()
+
+    small[0].wait()
+    small[1].wait()
+    floats = tokens[...].astype(f32)
+    values = (
+        floats
+        * lax.rsqrt(jnp.mean(floats * floats, axis=1, keepdims=True) + eps_norm)
+        * gain[...].reshape(1, width)
+    ).astype(bf16)
+    for n in range(nz):
+        normed[n] = values[:, n * depth : (n + 1) * depth]
+    at_me = pl.ds(pl.multiple_of((z * 2 + c) * rows, rows), rows)
+    xs[at_me, :] = normed[z]
+    small[2].wait()
+    flat = q_flat[...]
+    for n in range(q_flat.shape[0] // HD):
+        biases[x, n] = flat[n * HD : (n + 1) * HD].reshape(1, HD)
+    small[3].wait()
+    small[4].wait()
+
+    pl.semaphore_wait(barrier, len(friends))
+
+    def home_send(j, s, cc):
+        here = block(x, j, s)
+        for to, ssem, relayed in ((x_peer, w_send.at[0], cc == 1), (y_peer, w_send.at[1], cc == 0)):
+            go(here, here, ssem, w_relay.at[j], to, relayed)
+            go(here, here, ssem, w_rest.at[j], to, jnp.logical_not(relayed))
+
+    def own_block(j):
+        loaded(j)
+        go(stage.at[j], block(x, j, mine), w_send.at[2], w_home.at[j], core_peer)
+        home_send(j, mine, c)
+
+    def home(j):
+        got(blocks_like(1), w_home.at[j])
+        home_send(j, y * 2 + 1 - c, 1 - c)
+
+    def relay_weights(j):
+        got(blocks_like(2), w_relay.at[j])
+        here = block(x, j, (1 - y) * 2)
+        go(here, here, w_send.at[0], w_rest.at[j], x_peer)
+        here = block(1 - x, j, y * 2 + 1)
+        go(here, here, w_send.at[1], w_rest.at[j], y_peer)
+
+    at_end(w.at[pl.ds(0, 3), :, pl.ds(0, 2 * HD)], w_send.at[0])
+    at_end(w.at[pl.ds(0, 3), :, pl.ds(0, 2 * HD)], w_send.at[1])
+    at_end(blocks_like(chunks), w_send.at[2])
+
+    def token_block(zz, cc):
+        return xs.at[pl.ds(pl.multiple_of((zz * 2 + cc) * rows, rows), rows)]
+
+    def tokens_like(n):
+        return xs.at[pl.ds(0, n * rows)]
+
+    def send_tokens():
+        for to in (far, near, pair):
+            go(normed.at[to], token_block(z, c), x_send.at[0], x_recv.at[z], dev(to, y, c, x))
+        go(normed.at[z], token_block(z, c), x_send.at[1], x_recv.at[nz], core_peer)
+
+    def pass_tokens(zz):
+        here = token_block(zz, c)
+        got(here, x_recv.at[zz])
+        go(here, here, x_send.at[1], x_recv.at[nz], core_peer)
+
+    def wait_tokens():
+        got(tokens_like(nz), x_recv.at[nz])
+
+    at_end(tokens_like(nz - 1), x_send.at[0])
+    at_end(tokens_like(nz), x_send.at[1])
+
+    def send_biases():
+        go(biases.at[x], biases.at[x], b_sem.at[0], b_sem.at[1], x_peer)
+
+    held = xs.shape[0]
+    part_rows = held // p_recv.shape[2]
+
+    def shard(s):
+        return pl.ds(pl.multiple_of(s * HD, HD), HD)
+
+    def part_go(j, n, k, to, there):
+        at = pl.ds(n * part_rows, part_rows)
+        go(
+            part_out.at[j, k, at],
+            part_in.at[j, there, at],
+            p_send.at[0],
+            p_recv.at[j, there, n],
+            dev(to, y, c, x),
+        )
+
+    def part_got(j, n, k):
+        got(part_in.at[j, k, pl.ds(n * part_rows, part_rows)], p_recv.at[j, k, n])
+
+    def multiply(j):
+        got(blocks_like(4), w_rest.at[j])
+        full[j] = jnp.dot(xs[...], w[j], preferred_element_type=f32)
+
+        def send():
+            for k, s in enumerate((far, near, pair)):
+                for n in range(p_recv.shape[2]):
+                    at = pl.ds(n * part_rows, part_rows)
+                    part_out[j, k, at] = full[j, at, shard(s)].astype(bf16)
+                    part_go(j, n, k, pair, k)
+
+        pl.when(outer)(send)
+
+    def chain(j, steps):
+        def act():
+            for k, s, source, to, there in steps:
+                for n in range(p_recv.shape[2]):
+                    at = pl.ds(n * part_rows, part_rows)
+                    part_got(j, n, source)
+                    part_out[j, k, at] = (
+                        full[j, at, shard(s)] + part_in[j, source, at].astype(f32)
+                    ).astype(bf16)
+                    part_go(j, n, k, to, there)
+
+        pl.when(inner)(act)
+
+    def inward(j):
+        chain(j, ((0, far, 0, near, 3), (1, near, 1, near, 4)))
+
+    def outward(j):
+        chain(j, ((2, pair, 3, pair, 2),))
+
+    def summed(j):
+        def more():
+            for n in range(p_recv.shape[2]):
+                part_got(j, n, 4)
+            full[j, :, shard(z)] = full[j, :, shard(z)] + part_in[j, 4].astype(f32)
+
+        pl.when(inner)(more)
+        for n in range(p_recv.shape[2]):
+            part_got(j, n, 2)
+        return full[j, :, shard(z)] + part_in[j, 2].astype(f32)
+
+    at_end(part_out, p_send.at[0])
+
+    def turn(values):
+        return values * cosine[...] + pltpu.roll(values, HD // 2, 1) * sine[...]
+
+    here_src = y * 2 + x
+    others = [(1 - y) * 2 + x, y * 2 + 1 - x, (1 - y) * 2 + 1 - x]
+
+    def make_tables():
+        signs = jnp.where(lax.broadcasted_iota(jnp.int32, (1, HD), 1) < HD // 2, -1.0, 1.0)
+        cos_in, sin_in = base_cos_ref[2 * nz :], base_sin_ref[2 * nz :]
+        for n in range(2 * nz):
+            cos_at, sin_at = base_cos_ref[n : n + 1], base_sin_ref[n : n + 1]
+            cosine[n * rows : (n + 1) * rows] = cos_at * cos_in - sin_at * sin_in
+            sine[n * rows : (n + 1) * rows] = (sin_at * cos_in + cos_at * sin_in) * signs
+        at = lax.broadcasted_iota(jnp.int32, (2 * rows, 8 * rows), 1)
+        within = at % (2 * rows)
+        key_at = (
+            (at // (4 * rows)) * 4 + (within // rows) * 2 + (at // (2 * rows)) % 2
+        ) * rows + within % rows
+        at = lax.broadcasted_iota(jnp.int32, (2 * rows, 8 * rows), 0)
+        query_at = (y * 4 + (at // rows) * 2 + x) * rows + at % rows
+        hidden[...] = jnp.where(key_at <= query_at, 0.0, masked_score)
+
+    def make_kv():
+        at_group = pl.ds(pl.multiple_of(z * HD, HD), HD)
+        total = summed(0)
+        kv[c, here_src] = jnp.where(
+            c == 0, turn(total + k_bias[:, at_group]), total + v_bias[:, at_group]
+        ).astype(bf16)
+        here = kv.at[c, here_src]
+        go(here, here, kv_send.at[0], kv_recv.at[0], x_peer)
+        go(here, here, kv_send.at[0], kv_recv.at[1], y_peer)
+        go(here, here, kv_send.at[0], kv_recv.at[2], diagonal)
+        go(here, here, kv_send.at[1], kv_recv.at[3], core_peer)
+
+    def kv_pass():
+        for n, s in ((0, others[1]), (1, others[0]), (2, others[2])):
+            here = kv.at[c, s]
+            got(here, kv_recv.at[n])
+            go(here, here, kv_send.at[1], kv_recv.at[3], core_peer)
+
+    def kv_peer():
+        got(kv.at[0], kv_recv.at[3])
+        got(biases.at[1 - x], b_sem.at[1])
+
+    at_end(kv.at[0, pl.ds(0, 3)], kv_send.at[0])
+    at_end(kv.at[0], kv_send.at[1])
+    at_end(biases.at[0], b_sem.at[0])
+
+    factor = math.log2(math.e) / math.sqrt(HD)
+
+    def att_piece(h, zz, cc):
+        return att.at[h, :, pl.ds(pl.multiple_of((zz * 2 + cc) * HD, HD), HD)]
+
+    def attend(h):
+        total = summed(h + 1) + biases[zh, (z % 2) * G + c * per_core + h]
+        query = turn(total).astype(bf16)
+        cols_of_me = pl.ds(pl.multiple_of((z * 2 + c) * HD, HD), HD)
+        for t in range(nz):
+            q = query[t * 2 * rows : (t + 1) * 2 * rows]
+            scores = []
+            for u in range(t + 1):
+                keys = kv[0, :, u * 2 * rows : (u + 1) * 2 * rows].reshape(8 * rows, HD)
+                one = lax.dot_general(
+                    q, keys, (((1,), (1,)), ((), ())), preferred_element_type=f32
+                )
+                scores.append(one + hidden[...] if u == t else one)
+            top = jnp.max(functools.reduce(jnp.maximum, scores), axis=1, keepdims=True)
+            mixed, sums = None, None
+            for u in range(t + 1):
+                weights = jnp.exp2((scores[u] - top) * factor)
+                sums = weights if sums is None else sums + weights
+                vals = kv[1, :, u * 2 * rows : (u + 1) * 2 * rows].reshape(8 * rows, HD)
+                one = jnp.dot(weights.astype(bf16), vals, preferred_element_type=f32)
+                mixed = one if mixed is None else mixed + one
+            mixed = (mixed / jnp.sum(sums, axis=1, keepdims=True)).astype(bf16)
+            low, high = mixed[:rows], mixed[rows:]
+            att[h, t * rows : (t + 1) * rows, cols_of_me] = jnp.where(c == 0, low, high)
+            att_other[h, t * rows : (t + 1) * rows, :] = jnp.where(c == 0, high, low)
+        here, there = att_piece(h, z, c), att_other.at[h]
+        go(here, here, a_send.at[0], a_recv.at[h, z], dev(near, y, c, x), inner)
+        go(there, here, a_send.at[0], a_recv.at[h, z], dev(near, y, 1 - c, x), inner)
+        go(here, here, a_send.at[1], a_recv.at[h, z], dev(pair, y, c, x))
+        go(there, here, a_send.at[1], a_recv.at[h, z], dev(pair, y, 1 - c, x))
+        go(there, here, a_send.at[2], a_recv.at[h, z], core_peer)
+
+    def att_like(n):
+        return att.at[0, :, pl.ds(0, n * HD)]
+
+    def relay_attended(h, zz, to):
+        def act():
+            got(att_like(2), a_recv.at[h, zz])
+            for cc in range(2):
+                here = att_piece(h, zz, cc)
+                go(here, here, a_send.at[3], a_recv.at[h, zz], dev(to, y, c, x))
+
+        pl.when(inner)(act)
+
+    def from_near(h):
+        relay_attended(h, near, pair)
+
+    def from_pair(h):
+        relay_attended(h, pair, near)
+
+    def from_far(h):
+        relay_attended(h, far, pair)
+
+    def gathered(h):
+        def act():
+            for zz in (pair, near, far):
+                got(att_like(2), a_recv.at[h, zz])
+
+        pl.when(outer)(act)
+
+    at_end(att.at[:, :, pl.ds(0, 2 * HD)], a_send.at[0], inner)
+    at_end(att.at[:, :, pl.ds(0, 2 * HD)], a_send.at[1])
+    at_end(att.at[:, :, pl.ds(0, HD)], a_send.at[2])
+    at_end(att.at[:, :, pl.ds(0, 6 * HD)], a_send.at[3], inner)
+
+    def wo_go(h, xx, s, half, n, rsem, to):
+        here = wo_block(h, xx, s, half)
+        go(here, here, wo_send.at[n], rsem, to)
+
+    def wo_begin(h):
+        like = wo.at[h, pl.ds(0, each), pl.ds(0, wo_cols)]
+        pltpu.make_async_copy(like, like, wo_load_sem.at[h]).wait()
+        for half in range(2):
+            for n, to in enumerate((x_peer, y_peer, core_peer)):
+                wo_go(h, x, y * 2 + c, half, n, wo_recv.at[h, n], to)
+
+    def wo_relay(h):
+        got(wo_like(2), wo_recv.at[h, 1])
+        wo_go(h, x, (1 - y) * 2 + c, 0, 0, wo_recv.at[h, 3], x_peer)
+        got(wo_like(2), wo_recv.at[h, 0])
+        wo_go(h, 1 - x, y * 2 + c, 1, 1, wo_recv.at[h, 3], y_peer)
+        for half in range(2):
+            wo_go(h, x, (1 - y) * 2 + c, half, 2, wo_recv.at[h, 2], core_peer)
+            wo_go(h, 1 - x, y * 2 + c, half, 2, wo_recv.at[h, 2], core_peer)
+
+    def wo_finish(h):
+        got(wo_like(2), wo_recv.at[h, 3])
+        for half in range(2):
+            wo_go(h, 1 - x, (1 - y) * 2 + c, half, 2, wo_recv.at[h, 2], core_peer)
+
+    def wo_wait(h):
+        got(wo_like(8), wo_recv.at[h, 2])
+
+    at_end(wo.at[:, pl.ds(0, 3 * half_rows), pl.ds(0, wo_cols)], wo_send.at[0])
+    at_end(wo.at[:, pl.ds(0, 3 * half_rows), pl.ds(0, wo_cols)], wo_send.at[1])
+    at_end(wo.at[:, pl.ds(0, 8 * half_rows), pl.ds(0, wo_cols)], wo_send.at[2])
+
+    def produce(h):
+        wo_wait(h)
+        gathered(h)
+        got(att_like(1), a_recv.at[h, z])
+        for first in range(0, columns, 512):
+            size = min(512, columns - first)
+            part = lax.dot_general(
+                att[h], wo[h, first : first + size, :], (((1,), (1,)), ((), ())), preferred_element_type=f32
+            )
+            if h:
+                part = part + acc[:, first : first + size]
+            if h < per_core - 1:
+                acc[:, first : first + size] = part
+            else:
+                for t in range(nz):
+                    outs[t, :, first : first + size] = part[t * rows : (t + 1) * rows].astype(bf16)
+
+    def result_cols(zz):
+        return pl.ds(pl.multiple_of(zz * columns, HD), columns)
+
+    def last():
+        for d in range(1, nz):
+            to = (z + d) % nz
+            go(outs.at[to], result.at[:, result_cols(z)], o_sem.at[0], o_sem.at[1], dev(to, y, c, x))
+
+    at_end(outs.at[pl.ds(0, nz - 1)], o_sem.at[0])
+
+    send_tokens()
+    own_block(0)
+    send_biases()
+    home(0)
+    own_block(1)
+    make_tables()
+    relay_weights(0)
+    home(1)
+    own_block(2)
+    pass_tokens(pair)
+    pass_tokens(near)
+    pass_tokens(far)
+    wait_tokens()
+    multiply(0)
+    relay_weights(1)
+    home(2)
+    own_block(3)
+    inward(0)
+    home(3)
+    multiply(1)
+    relay_weights(2)
+    outward(0)
+    make_kv()
+    inward(1)
+    multiply(2)
+    outward(1)
+    relay_weights(3)
+    kv_pass()
+    kv_peer()
+    attend(0)
+    inward(2)
+    outward(2)
+    multiply(3)
+    from_pair(0)
+    inward(3)
+    from_near(0)
+    wo_begin(0)
+    attend(1)
+    outward(3)
+    from_far(0)
+    wo_begin(1)
+    from_pair(1)
+    attend(2)
+    from_near(1)
+    wo_relay(0)
+    wo_begin(2)
+    from_far(1)
+    from_pair(2)
+    wo_finish(0)
+    wo_relay(1)
+    from_near(2)
+    produce(0)
+    wo_finish(1)
+    wo_relay(2)
+    from_far(2)
+    produce(1)
+    wo_finish(2)
+    produce(2)
+    last()
+    out_ref[:, result_cols(z)] = outs[z]
+    for done in final_waits:
+        done()
+    got(outs.at[pl.ds(0, nz - 1)], o_sem.at[1])
+    for d in range(1, nz):
+        zz = (z + d) % nz
+        out_ref[:, result_cols(zz)] = result[:, result_cols(zz)]
+
+
+def in_planes(tokens, norm_gain, w_query, w_key, w_value, q_bias, k_bias, v_bias, w_out):
+    blocks = lax.axis_size("blk")
+    nz = blocks // 4
+    rows, width = tokens.shape
+    me, x = lax.axis_index("blk"), lax.axis_index("head")
+    inner, each, per_core = w_query.shape[1], w_query.shape[0], G // 2
+    chunks, held, columns = per_core + 1, 2 * nz * rows, width // nz
+    where = jnp.arange(2 * nz, dtype=jnp.int32)
+    there = (where // 2) * 4 + ((me // 2) % 2) * 2 + where % 2
+    positions = jnp.concatenate([(there * 2 + x) * rows, jnp.arange(rows, dtype=jnp.int32)])
+    half = HD // 2
+    lanes = jnp.arange(HD, dtype=jnp.int32) % half
+    freq = theta_base ** (-(lanes.astype(jnp.float32) * 2.0 / HD))
+    angles = positions.astype(jnp.float32)[:, None] * freq[None, :]
+    base_cos, base_sin = jnp.cos(angles), jnp.sin(angles)
+    vmem = pl.BlockSpec(memory_space=pltpu.VMEM)
+    hbm = pl.BlockSpec(memory_space=pltpu.HBM)
+    bf16, f32 = jnp.bfloat16, jnp.float32
+    dma = pltpu.SemaphoreType.DMA
+    return pl.pallas_call(
+        functools.partial(plane_kernel, nz),
+        out_shape=jax.ShapeDtypeStruct((rows, width), bf16),
+        in_specs=[hbm] * 9 + [vmem] * 2,
+        out_specs=vmem,
+        scratch_shapes=[
+            pltpu.VMEM((rows, width), bf16),
+            pltpu.VMEM((width,), f32),
+            pltpu.VMEM((inner,), f32),
+            pltpu.VMEM((1, w_key.shape[1]), f32),
+            pltpu.VMEM((1, w_key.shape[1]), f32),
+            pltpu.VMEM((held, HD), f32),
+            pltpu.VMEM((held, HD), f32),
+            pltpu.VMEM((chunks, each, 2 * HD), bf16),
+            pltpu.VMEM((chunks, 4 * each, 4 * HD), bf16),
+            pltpu.VMEM((nz, rows, width // nz), bf16),
+            pltpu.VMEM((held, width // nz), bf16),
+            pltpu.VMEM((chunks, 3, held, HD), bf16),
+            pltpu.VMEM((chunks, 5, held, HD), bf16),
+            pltpu.VMEM((chunks, held, 4 * HD), f32),
+            pltpu.VMEM((2, inner // HD, 1, HD), f32),
+            pltpu.VMEM((2, 4, held, HD), bf16),
+            pltpu.VMEM((2 * rows, 8 * rows), f32),
+            pltpu.VMEM((per_core, nz * rows, 2 * nz * HD), bf16),
+            pltpu.VMEM((per_core, nz * rows, HD), bf16),
+            pltpu.VMEM((per_core, columns, 2 * nz * HD), bf16),
+            pltpu.VMEM((nz * rows, columns), f32),
+            pltpu.VMEM((nz, rows, columns), bf16),
+            pltpu.VMEM((rows, width), bf16),
+            dma((5,)),
+            dma((chunks,)),
+            dma((per_core,)),
+            dma((3,)),
+            dma((chunks,)),
+            dma((chunks,)),
+            dma((chunks,)),
+            dma((2,)),
+            dma((nz + 1,)),
+            dma((2,)),
+            dma((1,)),
+            dma((chunks, 5, 2)),
+            dma((2,)),
+            dma((4,)),
+            dma((4,)),
+            dma((per_core, nz)),
+            dma((3,)),
+            dma((per_core, 4)),
+            dma((2,)),
+        ],
+        compiler_params=pltpu.CompilerParams(
+            collective_id=1, has_side_effects=True, vmem_limit_bytes=63 * 1024 * 1024
+        ),
+    )(
+        tokens,
+        norm_gain,
+        w_query,
+        w_key,
+        w_value,
+        q_bias,
+        k_bias[None, :],
+        v_bias[None, :],
+        w_out.T,
+        base_cos,
+        base_sin,
+    )
+
+
+def by_mesh(tokens, norm_gain, w_query, w_key, *rest):
+    blocks, heads = lax.axis_size("blk"), lax.axis_size("head")
+    groups = w_key.shape[1] // HD
+    fits = blocks == 16 and heads == 2 and groups == 4 and w_query.shape[1] == 2 * G * HD
+    run = in_planes if fits else on_device
+    return run(tokens, norm_gain, w_query, w_key, *rest)
+
+
 def solution(mesh):
     placed = (
         P(("blk", "head"), None),
@@ -523,5 +1179,5 @@
         P("head", "blk"),
     )
     return jax.shard_map(
-        on_device, mesh=mesh, in_specs=placed, out_specs=P(("blk", "head"), None), check_vma=False
+        by_mesh, mesh=mesh, in_specs=placed, out_specs=P(("blk", "head"), None), check_vma=False
     )

time: 161 us -> 98.5 us (0.61)
  Pallas kernels: 156 us -> 95.5 us
  local copies, waits for them, and re-layouts: 3.7 us -> 1.82 us
    pallas_call x1, Pallas kernels: 156 us -> 95.5 us  [in_planes(): pl.pallas_call(functools.partial(plane_kernel, nz), out_shape=jax.ShapeDt...]
where the time goes in v2:
time: 98.5 us; the launch traced here: 98.3 us
  Pallas kernels  95.5 us (97%)
  local copies, waits for them, and re-layouts  1.82 us (2%)
    pallas_call x1, Pallas kernels, in_planes(): pl.pallas_call(functools.partial(plane_kernel, nz), out_shape=jax.ShapeDt...  95.5 us

profile of v2, /device:TPU:0, one launch (start us, length us, event | category | flops | bytes accessed | tf_op | source)
XLA Modules:
  0.0 98.3 jit_solution(8617847616382073067)
XLA Ops:
  0.0 0.1 add_convert_fusion
  0.1 0.8 multiply_sine_fusion
  0.9 95.5 %shard_map.91 = bf16[64,3584]{1,0:T(8,128)(2,1)} custom-call(bf16[64,3584]{1,0:T(8,128)(2,1)} %tokens_ref.1, f32[3584]{0:T(1024)} %gain_ref.1, bf16[224,1536]{1,0:T(8,128)(2,1)} %w_query_ref.1, bf16[224,512]{1,0:T(8,128)(2,1)} %w_key_ref.1, bf16[224,512]{1,0:T(8,128)(2,1)} %w_value_ref.1, f32[1536]{0:T(1024)} %q_bias_ref.1, f32[1,512]{1,0:T(1,128)} %bitcast.4, ...), custom_call_target="tpu_custom_call" | custom-call | tf_op jit(solution)/shard_map/pallas_call | solution.py:1094
  96.5 1.8 %copy.11 = bf16[64,3584]{1,0:T(8,128)(2,1)} copy(bf16[64,3584]{1,0:T(8,128)(2,1)} %shard_map.91) | data formatting | bytes 917504
  (3 shorter events, 0.0 us)

commit v3 on v2

--- a/solution.py
+++ b/solution.py
@@ -3,6 +3,7 @@
 
 import jax
 import jax.numpy as jnp
+import numpy as np
 from jax import lax
 from jax.experimental import pallas as pl
 from jax.experimental.pallas import tpu as pltpu
@@ -525,6 +526,8 @@
     base_sin_ref,
     out_ref,
     tokens,
+    base_cos,
+    base_sin,
     gain,
     q_flat,
     k_bias,
@@ -583,6 +586,12 @@
     pair = z + 1 - 2 * (z % 2)
     near, far = 2 - zh, 3 - 3 * zh
     final_waits = []
+    order = (0, nz - 1) + tuple(range(1, nz - 1))
+    halves = 2
+    span = nz // halves * 2 * rows
+
+    def spot(zz):
+        return jnp.where(((zz + 1) // 2) % 2 == 1, zz + 1, zz // 3)
 
     def dev(zz, yy, cc, xx):
         return ((zz * 2 + yy) * 2 + cc, xx)
@@ -621,6 +630,8 @@
         pltpu.make_async_copy(q_bias_ref, q_flat, small_sem.at[2]),
         pltpu.make_async_copy(k_bias_ref, k_bias, small_sem.at[3]),
         pltpu.make_async_copy(v_bias_ref, v_bias, small_sem.at[4]),
+        pltpu.make_async_copy(base_cos_ref, base_cos, small_sem.at[5]),
+        pltpu.make_async_copy(base_sin_ref, base_sin, small_sem.at[6]),
     ]
     for one in small:
         one.start()
@@ -701,7 +712,7 @@
     ).astype(bf16)
     for n in range(nz):
         normed[n] = values[:, n * depth : (n + 1) * depth]
-    at_me = pl.ds(pl.multiple_of((z * 2 + c) * rows, rows), rows)
+    at_me = pl.ds(pl.multiple_of((spot(z) * 2 + c) * rows, rows), rows)
     xs[at_me, :] = normed[z]
     small[2].wait()
     flat = q_flat[...]
@@ -709,13 +720,15 @@
         biases[x, n] = flat[n * HD : (n + 1) * HD].reshape(1, HD)
     small[3].wait()
     small[4].wait()
+    small[5].wait()
+    small[6].wait()
 
     pl.semaphore_wait(barrier, len(friends))
 
     def home_send(j, s, cc):
         here = block(x, j, s)
         for to, ssem, relayed in ((x_peer, w_send.at[0], cc == 1), (y_peer, w_send.at[1], cc == 0)):
-            go(here, here, ssem, w_relay.at[j], to, relayed)
+            go(here, here, ssem, w_relay.at[j, 1 if to is x_peer else 0], to, relayed)
             go(here, here, ssem, w_rest.at[j], to, jnp.logical_not(relayed))
 
     def own_block(j):
@@ -727,19 +740,26 @@
         got(blocks_like(1), w_home.at[j])
         home_send(j, y * 2 + 1 - c, 1 - c)
 
-    def relay_weights(j):
-        got(blocks_like(2), w_relay.at[j])
-        here = block(x, j, (1 - y) * 2)
-        go(here, here, w_send.at[0], w_rest.at[j], x_peer)
-        here = block(1 - x, j, y * 2 + 1)
-        go(here, here, w_send.at[1], w_rest.at[j], y_peer)
+    def relay_weights(j, k):
+        def from_y():
+            got(blocks_like(1), w_relay.at[j, 0])
+            here = block(x, j, (1 - y) * 2)
+            go(here, here, w_send.at[0], w_rest.at[j], x_peer)
+
+        def from_x():
+            got(blocks_like(1), w_relay.at[j, 1])
+            here = block(1 - x, j, y * 2 + 1)
+            go(here, here, w_send.at[1], w_rest.at[j], y_peer)
+
+        pl.when(c == k)(from_y)
+        pl.when(c != k)(from_x)
 
     at_end(w.at[pl.ds(0, 3), :, pl.ds(0, 2 * HD)], w_send.at[0])
     at_end(w.at[pl.ds(0, 3), :, pl.ds(0, 2 * HD)], w_send.at[1])
     at_end(blocks_like(chunks), w_send.at[2])
 
     def token_block(zz, cc):
-        return xs.at[pl.ds(pl.multiple_of((zz * 2 + cc) * rows, rows), rows)]
+        return xs.at[pl.ds(pl.multiple_of((spot(zz) * 2 + cc) * rows, rows), rows)]
 
     def tokens_like(n):
         return xs.at[pl.ds(0, n * rows)]
@@ -763,81 +783,79 @@
     def send_biases():
         go(biases.at[x], biases.at[x], b_sem.at[0], b_sem.at[1], x_peer)
 
-    held = xs.shape[0]
-    part_rows = held // p_recv.shape[2]
-
     def shard(s):
         return pl.ds(pl.multiple_of(s * HD, HD), HD)
 
+    def half_at(n):
+        return pl.ds(n * span, span)
+
     def part_go(j, n, k, to, there):
-        at = pl.ds(n * part_rows, part_rows)
         go(
-            part_out.at[j, k, at],
-            part_in.at[j, there, at],
+            part_out.at[j, k, half_at(n)],
+            part_in.at[j, there, half_at(n)],
             p_send.at[0],
             p_recv.at[j, there, n],
             dev(to, y, c, x),
         )
 
     def part_got(j, n, k):
-        got(part_in.at[j, k, pl.ds(n * part_rows, part_rows)], p_recv.at[j, k, n])
+        got(part_in.at[j, k, half_at(n)], p_recv.at[j, k, n])
 
     def multiply(j):
         got(blocks_like(4), w_rest.at[j])
         full[j] = jnp.dot(xs[...], w[j], preferred_element_type=f32)
 
         def send():
-            for k, s in enumerate((far, near, pair)):
-                for n in range(p_recv.shape[2]):
-                    at = pl.ds(n * part_rows, part_rows)
-                    part_out[j, k, at] = full[j, at, shard(s)].astype(bf16)
+            for n in range(halves):
+                for k, s in enumerate((far, near, pair)):
+                    part_out[j, k, half_at(n)] = full[j, half_at(n), shard(s)].astype(bf16)
                     part_go(j, n, k, pair, k)
 
         pl.when(outer)(send)
 
-    def chain(j, steps):
+    def chain(j, n, steps):
         def act():
             for k, s, source, to, there in steps:
-                for n in range(p_recv.shape[2]):
-                    at = pl.ds(n * part_rows, part_rows)
-                    part_got(j, n, source)
-                    part_out[j, k, at] = (
-                        full[j, at, shard(s)] + part_in[j, source, at].astype(f32)
-                    ).astype(bf16)
-                    part_go(j, n, k, to, there)
+                part_got(j, n, source)
+                part_out[j, k, half_at(n)] = (
+                    full[j, half_at(n), shard(s)] + part_in[j, source, half_at(n)].astype(f32)
+                ).astype(bf16)
+                part_go(j, n, k, to, there)
 
         pl.when(inner)(act)
 
-    def inward(j):
-        chain(j, ((0, far, 0, near, 3), (1, near, 1, near, 4)))
-
-    def outward(j):
-        chain(j, ((2, pair, 3, pair, 2),))
-
-    def summed(j):
+    def inward(j, n):
+        chain(j, n, ((0, far, 0, near, 3), (1, near, 1, near, 4)))
+
+    def outward(j, n):
+        chain(j, n, ((2, pair, 3, pair, 2),))
+
+    def summed(j, n):
         def more():
-            for n in range(p_recv.shape[2]):
-                part_got(j, n, 4)
-            full[j, :, shard(z)] = full[j, :, shard(z)] + part_in[j, 4].astype(f32)
+            part_got(j, n, 4)
+            full[j, half_at(n), shard(z)] = (
+                full[j, half_at(n), shard(z)] + part_in[j, 4, half_at(n)].astype(f32)
+            )
 
         pl.when(inner)(more)
-        for n in range(p_recv.shape[2]):
-            part_got(j, n, 2)
-        return full[j, :, shard(z)] + part_in[j, 2].astype(f32)
+        part_got(j, n, 2)
+        return full[j, half_at(n), shard(z)] + part_in[j, 2, half_at(n)].astype(f32)
 
     at_end(part_out, p_send.at[0])
 
-    def turn(values):
-        return values * cosine[...] + pltpu.roll(values, HD // 2, 1) * sine[...]
+    def turn(values, n):
+        return values * cosine[half_at(n)] + pltpu.roll(values, HD // 2, 1) * sine[half_at(n)]
 
     here_src = y * 2 + x
     others = [(1 - y) * 2 + x, y * 2 + 1 - x, (1 - y) * 2 + 1 - x]
 
     def make_tables():
         signs = jnp.where(lax.broadcasted_iota(jnp.int32, (1, HD), 1) < HD // 2, -1.0, 1.0)
-        cos_in, sin_in = base_cos_ref[2 * nz :], base_sin_ref[2 * nz :]
+        starts = base_cos.shape[0] - rows
+        cos_in, sin_in = base_cos[starts:], base_sin[starts:]
         for n in range(2 * nz):
-            cos_at, sin_at = base_cos_ref[n : n + 1], base_sin_ref[n : n + 1]
+            row = pl.ds((order[n // 2] * 4 + y * 2 + n % 2) * 2 + x, 1)
+            cos_at, sin_at = base_cos[row], base_sin[row]
             cosine[n * rows : (n + 1) * rows] = cos_at * cos_in - sin_at * sin_in
             sine[n * rows : (n + 1) * rows] = (sin_at * cos_in + cos_at * sin_in) * signs
         at = lax.broadcasted_iota(jnp.int32, (2 * rows, 8 * rows), 1)
@@ -849,26 +867,29 @@
         query_at = (y * 4 + (at // rows) * 2 + x) * rows + at % rows
         hidden[...] = jnp.where(key_at <= query_at, 0.0, masked_score)
 
-    def make_kv():
+    def kv_half(kind, s, n):
+        return kv.at[kind, s, half_at(n)]
+
+    def make_kv(n):
         at_group = pl.ds(pl.multiple_of(z * HD, HD), HD)
-        total = summed(0)
-        kv[c, here_src] = jnp.where(
-            c == 0, turn(total + k_bias[:, at_group]), total + v_bias[:, at_group]
+        total = summed(0, n)
+        kv[c, here_src, half_at(n)] = jnp.where(
+            c == 0, turn(total + k_bias[:, at_group], n), total + v_bias[:, at_group]
         ).astype(bf16)
-        here = kv.at[c, here_src]
-        go(here, here, kv_send.at[0], kv_recv.at[0], x_peer)
-        go(here, here, kv_send.at[0], kv_recv.at[1], y_peer)
-        go(here, here, kv_send.at[0], kv_recv.at[2], diagonal)
-        go(here, here, kv_send.at[1], kv_recv.at[3], core_peer)
-
-    def kv_pass():
-        for n, s in ((0, others[1]), (1, others[0]), (2, others[2])):
-            here = kv.at[c, s]
-            got(here, kv_recv.at[n])
-            go(here, here, kv_send.at[1], kv_recv.at[3], core_peer)
+        here = kv_half(c, here_src, n)
+        go(here, here, kv_send.at[0], kv_recv.at[n], x_peer)
+        go(here, here, kv_send.at[0], kv_recv.at[2 + n], y_peer)
+        go(here, here, kv_send.at[0], kv_recv.at[4 + n], diagonal)
+        go(here, here, kv_send.at[1], kv_recv.at[6], core_peer)
+
+    def kv_pass(n):
+        for k, s in ((0, others[1]), (2, others[0]), (4, others[2])):
+            here = kv_half(c, s, n)
+            got(here, kv_recv.at[k + n])
+            go(here, here, kv_send.at[1], kv_recv.at[6], core_peer)
 
     def kv_peer():
-        got(kv.at[0], kv_recv.at[3])
+        got(kv.at[0], kv_recv.at[6])
         got(biases.at[1 - x], b_sem.at[1])
 
     at_end(kv.at[0, pl.ds(0, 3)], kv_send.at[0])
@@ -877,73 +898,103 @@
 
     factor = math.log2(math.e) / math.sqrt(HD)
 
-    def att_piece(h, zz, cc):
-        return att.at[h, :, pl.ds(pl.multiple_of((zz * 2 + cc) * HD, HD), HD)]
-
-    def attend(h):
-        total = summed(h + 1) + biases[zh, (z % 2) * G + c * per_core + h]
-        query = turn(total).astype(bf16)
+    att_rows = nz // halves * rows
+
+    def att_piece(h, n, zz, cc):
+        return att.at[
+            h,
+            pl.ds(n * att_rows, att_rows),
+            pl.ds(pl.multiple_of((zz * 2 + cc) * HD, HD), HD),
+        ]
+
+    def att_like(count):
+        return att.at[0, pl.ds(0, att_rows), pl.ds(0, count * HD)]
+
+    def attend(h, n):
+        total = summed(h + 1, n) + biases[zh, (z % 2) * G + c * per_core + h]
+        query = turn(total, n).astype(bf16)
         cols_of_me = pl.ds(pl.multiple_of((z * 2 + c) * HD, HD), HD)
-        for t in range(nz):
-            q = query[t * 2 * rows : (t + 1) * 2 * rows]
+        for k in range(nz // halves):
+            t = order[n * (nz // halves) + k]
+            q = query[k * 2 * rows : (k + 1) * 2 * rows]
+            tiles = [pl.ds(order.index(u) * 2 * rows, 2 * rows) for u in range(t + 1)]
             scores = []
-            for u in range(t + 1):
-                keys = kv[0, :, u * 2 * rows : (u + 1) * 2 * rows].reshape(8 * rows, HD)
-                one = lax.dot_general(
-                    q, keys, (((1,), (1,)), ((), ())), preferred_element_type=f32
+            for tile in tiles:
+                keys = kv[0, :, tile].reshape(8 * rows, HD)
+                scores.append(
+                    lax.dot_general(
+                        q, keys, (((1,), (1,)), ((), ())), preferred_element_type=f32
+                    )
                 )
-                scores.append(one + hidden[...] if u == t else one)
+            scores[t] = scores[t] + hidden[...]
             top = jnp.max(functools.reduce(jnp.maximum, scores), axis=1, keepdims=True)
             mixed, sums = None, None
-            for u in range(t + 1):
-                weights = jnp.exp2((scores[u] - top) * factor)
+            for tile, one in zip(tiles, scores):
+                weights = jnp.exp2((one - top) * factor)
                 sums = weights if sums is None else sums + weights
-                vals = kv[1, :, u * 2 * rows : (u + 1) * 2 * rows].reshape(8 * rows, HD)
+                vals = kv[1, :, tile].reshape(8 * rows, HD)
                 one = jnp.dot(weights.astype(bf16), vals, preferred_element_type=f32)
                 mixed = one if mixed is None else mixed + one
             mixed = (mixed / jnp.sum(sums, axis=1, keepdims=True)).astype(bf16)
             low, high = mixed[:rows], mixed[rows:]
-            att[h, t * rows : (t + 1) * rows, cols_of_me] = jnp.where(c == 0, low, high)
-            att_other[h, t * rows : (t + 1) * rows, :] = jnp.where(c == 0, high, low)
-        here, there = att_piece(h, z, c), att_other.at[h]
-        go(here, here, a_send.at[0], a_recv.at[h, z], dev(near, y, c, x), inner)
-        go(there, here, a_send.at[0], a_recv.at[h, z], dev(near, y, 1 - c, x), inner)
-        go(here, here, a_send.at[1], a_recv.at[h, z], dev(pair, y, c, x))
-        go(there, here, a_send.at[1], a_recv.at[h, z], dev(pair, y, 1 - c, x))
-        go(there, here, a_send.at[2], a_recv.at[h, z], core_peer)
-
-    def att_like(n):
-        return att.at[0, :, pl.ds(0, n * HD)]
-
-    def relay_attended(h, zz, to):
+            at = pl.ds(n * att_rows + k * rows, rows)
+            att[h, at, cols_of_me] = jnp.where(c == 0, low, high)
+            att_other[h, at, :] = jnp.where(c == 0, high, low)
+        here, there = att_piece(h, n, z, c), att_other.at[h, pl.ds(n * att_rows, att_rows)]
+        rsem = a_recv.at[h, n, z]
+        direct = (h, n) == (per_core - 1, halves - 1)
+
+        def att_go(k, to, when=None):
+            go(here, here, a_send.at[k], rsem, dev(to, y, c, x), when)
+            go(there, here, a_send.at[k], rsem, dev(to, y, 1 - c, x), when)
+
+        if direct:
+            att_go(4, far)
+            att_go(4, near)
+        else:
+            att_go(0, near, inner)
+        att_go(1, pair)
+        go(there, here, a_send.at[2], rsem, core_peer)
+
+    def relay_attended(h, n, zz, to):
         def act():
-            got(att_like(2), a_recv.at[h, zz])
+            got(att_like(2), a_recv.at[h, n, zz])
             for cc in range(2):
-                here = att_piece(h, zz, cc)
-                go(here, here, a_send.at[3], a_recv.at[h, zz], dev(to, y, c, x))
+                here = att_piece(h, n, zz, cc)
+                go(here, here, a_send.at[3], a_recv.at[h, n, zz], dev(to, y, c, x))
 
         pl.when(inner)(act)
 
-    def from_near(h):
-        relay_attended(h, near, pair)
-
-    def from_pair(h):
-        relay_attended(h, pair, near)
-
-    def from_far(h):
-        relay_attended(h, far, pair)
-
-    def gathered(h):
+    def from_near(h, n):
+        relay_attended(h, n, near, pair)
+
+    def from_pair(h, n):
+        relay_attended(h, n, pair, near)
+
+    def from_far(h, n):
+        relay_attended(h, n, far, pair)
+
+    def gathered(h, n):
         def act():
             for zz in (pair, near, far):
-                got(att_like(2), a_recv.at[h, zz])
-
-        pl.when(outer)(act)
-
-    at_end(att.at[:, :, pl.ds(0, 2 * HD)], a_send.at[0], inner)
+                got(att_like(2), a_recv.at[h, n, zz])
+
+        if (h, n) == (per_core - 1, halves - 1):
+            act()
+        else:
+            pl.when(outer)(act)
+        got(att_like(1), a_recv.at[h, n, z])
+
+    steps = per_core * halves
+
+    def att_sent(pieces):
+        return att.at[pl.ds(0, 2), pl.ds(0, pieces * att_rows // (4 * nz)), :]
+
+    at_end(att_sent(2 * (steps - 1)), a_send.at[0], inner)
+    at_end(att_sent(4), a_send.at[4])
     at_end(att.at[:, :, pl.ds(0, 2 * HD)], a_send.at[1])
     at_end(att.at[:, :, pl.ds(0, HD)], a_send.at[2])
-    at_end(att.at[:, :, pl.ds(0, 6 * HD)], a_send.at[3], inner)
+    at_end(att_sent(6 * (steps - 1)), a_send.at[3], inner)
 
     def wo_go(h, xx, s, half, n, rsem, to):
         here = wo_block(h, xx, s, half)
@@ -977,30 +1028,37 @@
     at_end(wo.at[:, pl.ds(0, 3 * half_rows), pl.ds(0, wo_cols)], wo_send.at[1])
     at_end(wo.at[:, pl.ds(0, 8 * half_rows), pl.ds(0, wo_cols)], wo_send.at[2])
 
-    def produce(h):
-        wo_wait(h)
-        gathered(h)
-        got(att_like(1), a_recv.at[h, z])
+    def produce(h, n):
+        gathered(h, n)
+        at = slice(n * att_rows, (n + 1) * att_rows)
         for first in range(0, columns, 512):
-            size = min(512, columns - first)
+            cols = slice(first, min(first + 512, columns))
             part = lax.dot_general(
-                att[h], wo[h, first : first + size, :], (((1,), (1,)), ((), ())), preferred_element_type=f32
+                att[h, at], wo[h, cols, :], (((1,), (1,)), ((), ())), preferred_element_type=f32
             )
             if h:
-                part = part + acc[:, first : first + size]
+                part = part + acc[at, cols]
             if h < per_core - 1:
-                acc[:, first : first + size] = part
+                acc[at, cols] = part
             else:
-                for t in range(nz):
-                    outs[t, :, first : first + size] = part[t * rows : (t + 1) * rows].astype(bf16)
+                for k in range(nz // halves):
+                    t = order[n * (nz // halves) + k]
+                    outs[t, :, cols] = part[k * rows : (k + 1) * rows].astype(bf16)
 
     def result_cols(zz):
         return pl.ds(pl.multiple_of(zz * columns, HD), columns)
 
-    def last():
-        for d in range(1, nz):
-            to = (z + d) % nz
-            go(outs.at[to], result.at[:, result_cols(z)], o_sem.at[0], o_sem.at[1], dev(to, y, c, x))
+    def last(n):
+        for k in range(nz // halves):
+            t = order[n * (nz // halves) + k]
+            go(
+                outs.at[t],
+                result.at[:, result_cols(z)],
+                o_sem.at[0],
+                o_sem.at[1],
+                dev(t, y, c, x),
+                z != t,
+            )
 
     at_end(outs.at[pl.ds(0, nz - 1)], o_sem.at[0])
 
@@ -1008,61 +1066,91 @@
     own_block(0)
     send_biases()
     home(0)
+    make_tables()
+    relay_weights(0, 0)
+    relay_weights(0, 1)
     own_block(1)
-    make_tables()
-    relay_weights(0)
     home(1)
-    own_block(2)
     pass_tokens(pair)
     pass_tokens(near)
     pass_tokens(far)
     wait_tokens()
     multiply(0)
-    relay_weights(1)
+    relay_weights(1, 0)
+    relay_weights(1, 1)
+    own_block(2)
     home(2)
+    inward(0, 0)
+    multiply(1)
+    outward(0, 0)
+    inward(0, 1)
+    relay_weights(2, 0)
+    relay_weights(2, 1)
+    make_kv(0)
+    outward(0, 1)
+    make_kv(1)
     own_block(3)
-    inward(0)
     home(3)
-    multiply(1)
-    relay_weights(2)
-    outward(0)
-    make_kv()
-    inward(1)
+    inward(1, 0)
     multiply(2)
-    outward(1)
-    relay_weights(3)
-    kv_pass()
+    outward(1, 0)
+    inward(1, 1)
+    outward(1, 1)
+    kv_pass(0)
+    inward(2, 0)
+    kv_pass(1)
     kv_peer()
-    attend(0)
-    inward(2)
-    outward(2)
+    attend(0, 0)
+    relay_weights(3, 0)
+    relay_weights(3, 1)
+    attend(0, 1)
+    wo_begin(0)
+    inward(2, 1)
+    from_near(0, 0)
+    outward(2, 0)
+    from_near(0, 1)
     multiply(3)
-    from_pair(0)
-    inward(3)
-    from_near(0)
-    wo_begin(0)
-    attend(1)
-    outward(3)
-    from_far(0)
     wo_begin(1)
-    from_pair(1)
-    attend(2)
-    from_near(1)
+    outward(2, 1)
+    from_pair(0, 0)
+    from_pair(0, 1)
+    attend(1, 0)
     wo_relay(0)
+    attend(1, 1)
+    inward(3, 0)
+    from_near(1, 0)
+    from_far(0, 0)
+    from_near(1, 1)
     wo_begin(2)
-    from_far(1)
-    from_pair(2)
+    outward(3, 0)
+    inward(3, 1)
+    from_far(0, 1)
+    wo_relay(1)
+    from_pair(1, 0)
+    outward(3, 1)
+    attend(2, 0)
+    from_pair(1, 1)
+    attend(2, 1)
     wo_finish(0)
-    wo_relay(1)
-    from_near(2)
-    produce(0)
+    from_far(1, 0)
+    from_near(2, 0)
+    from_far(1, 1)
+    wo_relay(2)
+    from_pair(2, 0)
     wo_finish(1)
-    wo_relay(2)
-    from_far(2)
-    produce(1)
+    wo_wait(0)
+    produce(0, 0)
+    produce(0, 1)
+    from_far(2, 0)
     wo_finish(2)
-    produce(2)
-    last()
+    wo_wait(1)
+    produce(1, 0)
+    produce(1, 1)
+    wo_wait(2)
+    produce(2, 0)
+    last(0)
+    produce(2, 1)
+    last(1)
     out_ref[:, result_cols(z)] = outs[z]
     for done in final_waits:
         done()
@@ -1076,17 +1164,13 @@
     blocks = lax.axis_size("blk")
     nz = blocks // 4
     rows, width = tokens.shape
-    me, x = lax.axis_index("blk"), lax.axis_index("head")
     inner, each, per_core = w_query.shape[1], w_query.shape[0], G // 2
     chunks, held, columns = per_core + 1, 2 * nz * rows, width // nz
-    where = jnp.arange(2 * nz, dtype=jnp.int32)
-    there = (where // 2) * 4 + ((me // 2) % 2) * 2 + where % 2
-    positions = jnp.concatenate([(there * 2 + x) * rows, jnp.arange(rows, dtype=jnp.int32)])
-    half = HD // 2
-    lanes = jnp.arange(HD, dtype=jnp.int32) % half
-    freq = theta_base ** (-(lanes.astype(jnp.float32) * 2.0 / HD))
-    angles = positions.astype(jnp.float32)[:, None] * freq[None, :]
-    base_cos, base_sin = jnp.cos(angles), jnp.sin(angles)
+    positions = np.concatenate([np.arange(2 * blocks) * rows, np.arange(rows)])
+    lanes = np.arange(HD) % (HD // 2)
+    angles = positions[:, None] * theta_base ** (-2.0 * lanes / HD)[None, :]
+    base_cos = jnp.asarray(np.cos(angles), jnp.float32)
+    base_sin = jnp.asarray(np.sin(angles), jnp.float32)
     vmem = pl.BlockSpec(memory_space=pltpu.VMEM)
     hbm = pl.BlockSpec(memory_space=pltpu.HBM)
     bf16, f32 = jnp.bfloat16, jnp.float32
@@ -1094,10 +1178,12 @@
     return pl.pallas_call(
         functools.partial(plane_kernel, nz),
         out_shape=jax.ShapeDtypeStruct((rows, width), bf16),
-        in_specs=[hbm] * 9 + [vmem] * 2,
+        in_specs=[hbm] * 11,
         out_specs=vmem,
         scratch_shapes=[
             pltpu.VMEM((rows, width), bf16),
+            pltpu.VMEM(base_cos.shape, f32),
+            pltpu.VMEM(base_sin.shape, f32),
             pltpu.VMEM((width,), f32),
             pltpu.VMEM((inner,), f32),
             pltpu.VMEM((1, w_key.shape[1]), f32),
@@ -1120,12 +1206,12 @@
             pltpu.VMEM((nz * rows, columns), f32),
             pltpu.VMEM((nz, rows, columns), bf16),
             pltpu.VMEM((rows, width), bf16),
-            dma((5,)),
+            dma((7,)),
             dma((chunks,)),
             dma((per_core,)),
             dma((3,)),
             dma((chunks,)),
-            dma((chunks,)),
+            dma((chunks, 2)),
             dma((chunks,)),
             dma((2,)),
             dma((nz + 1,)),
@@ -1133,9 +1219,9 @@
             dma((1,)),
             dma((chunks, 5, 2)),
             dma((2,)),
-            dma((4,)),
-            dma((4,)),
-            dma((per_core, nz)),
+            dma((7,)),
+            dma((5,)),
+            dma((per_core, 2, nz)),
             dma((3,)),
             dma((per_core, 4)),
             dma((2,)),

time: 98.5 us -> 91.1 us (0.925)
  Pallas kernels: 95.5 us -> 88.7 us
    pallas_call x1, Pallas kernels: 95.5 us -> 88.7 us  [in_planes(): pl.pallas_call(functools.partial(plane_kernel, nz), out_shape=jax.ShapeDt...]
where the time goes in v3:
time: 91.1 us; the launch traced here: 90.5 us
  Pallas kernels  88.7 us (97%)
  local copies, waits for them, and re-layouts  1.82 us (2%)
    pallas_call x1, Pallas kernels, in_planes(): pl.pallas_call(functools.partial(plane_kernel, nz), out_shape=jax.ShapeDt...  88.7 us

profile of v3, /device:TPU:0, one launch (start us, length us, event | category | flops | bytes accessed | tf_op | source)
XLA Modules:
  0.0 90.5 jit_solution(3042233159496695993)
XLA Ops:
  0.0 88.7 %shard_map.109 = bf16[64,3584]{1,0:T(8,128)(2,1)} custom-call(bf16[64,3584]{1,0:T(8,128)(2,1)} %tokens_ref.1, f32[3584]{0:T(1024)} %gain_ref.1, bf16[224,1536]{1,0:T(8,128)(2,1)} %w_query_ref.1, bf16[224,512]{1,0:T(8,128)(2,1)} %w_key_ref.1, bf16[224,512]{1,0:T(8,128)(2,1)} %w_value_ref.1, f32[1536]{0:T(1024)} %q_bias_ref.1, f32[1,512]{1,0:T(1,128)} %bitcast.4, ...), custom_call_target="tpu_custom_call" | custom-call | tf_op jit(solution)/shard_map/pallas_call | solution.py:1178
  88.7 1.8 %copy.13 = bf16[64,3584]{1,0:T(8,128)(2,1)} copy(bf16[64,3584]{1,0:T(8,128)(2,1)} %shard_map.109) | data formatting | bytes 917504

commit v4 on v3

--- a/solution.py
+++ b/solution.py
@@ -1086,10 +1086,10 @@
     inward(0, 1)
     relay_weights(2, 0)
     relay_weights(2, 1)
+    own_block(3)
     make_kv(0)
     outward(0, 1)
     make_kv(1)
-    own_block(3)
     home(3)
     inward(1, 0)
     multiply(2)
@@ -1116,37 +1116,37 @@
     from_pair(0, 1)
     attend(1, 0)
     wo_relay(0)
+    wo_begin(2)
     attend(1, 1)
     inward(3, 0)
     from_near(1, 0)
     from_far(0, 0)
     from_near(1, 1)
-    wo_begin(2)
     outward(3, 0)
     inward(3, 1)
     from_far(0, 1)
     wo_relay(1)
     from_pair(1, 0)
+    from_pair(1, 1)
     outward(3, 1)
     attend(2, 0)
-    from_pair(1, 1)
     attend(2, 1)
     wo_finish(0)
     from_far(1, 0)
+    wo_relay(2)
     from_near(2, 0)
+    wo_finish(1)
     from_far(1, 1)
-    wo_relay(2)
     from_pair(2, 0)
-    wo_finish(1)
     wo_wait(0)
     produce(0, 0)
     produce(0, 1)
-    from_far(2, 0)
-    wo_finish(2)
     wo_wait(1)
     produce(1, 0)
     produce(1, 1)
+    wo_finish(2)
     wo_wait(2)
+    from_far(2, 0)
     produce(2, 0)
     last(0)
     produce(2, 1)

time: 91.1 us -> 90.2 us (level)
  no operation moved by 1% of the time
where the time goes in v4:
time: 90.2 us; the launch traced here: 90 us
  Pallas kernels  88.2 us (98%)
  local copies, waits for them, and re-layouts  1.82 us (2%)
    pallas_call x1, Pallas kernels, in_planes(): pl.pallas_call(functools.partial(plane_kernel, nz), out_shape=jax.ShapeDt...  88.2 us
    unnamed x1, local copies, waits for them, and re-layouts  1.82 us

profile of v4, /device:TPU:0, one launch (start us, length us, event | category | flops | bytes accessed | tf_op | source)
XLA Modules:
  0.0 90.0 jit_solution(4348859803885075583)
XLA Ops:
  0.0 88.2 %shard_map.109 = bf16[64,3584]{1,0:T(8,128)(2,1)} custom-call(bf16[64,3584]{1,0:T(8,128)(2,1)} %tokens_ref.1, f32[3584]{0:T(1024)} %gain_ref.1, bf16[224,1536]{1,0:T(8,128)(2,1)} %w_query_ref.1, bf16[224,512]{1,0:T(8,128)(2,1)} %w_key_ref.1, bf16[224,512]{1,0:T(8,128)(2,1)} %w_value_ref.1, f32[1536]{0:T(1024)} %q_bias_ref.1, f32[1,512]{1,0:T(1,128)} %bitcast.4, ...), custom_call_target="tpu_custom_call" | custom-call | tf_op jit(solution)/shard_map/pallas_call | solution.py:1178
  88.2 1.8 %copy.13 = bf16[64,3584]{1,0:T(8,128)(2,1)} copy(bf16[64,3584]{1,0:T(8,128)(2,1)} %shard_map.109) | data formatting | bytes 917504

commit v5 on v4

--- a/solution.py
+++ b/solution.py
@@ -1098,11 +1098,11 @@
     outward(1, 1)
     kv_pass(0)
     inward(2, 0)
+    relay_weights(3, 0)
     kv_pass(1)
+    relay_weights(3, 1)
     kv_peer()
     attend(0, 0)
-    relay_weights(3, 0)
-    relay_weights(3, 1)
     attend(0, 1)
     wo_begin(0)
     inward(2, 1)

time: 90.2 us -> 93.2 us (1.033)
  Pallas kernels: 88.2 us -> 91.2 us
    pallas_call x1, Pallas kernels: 88.2 us -> 91.2 us  [in_planes(): pl.pallas_call(functools.partial(plane_kernel, nz), out_shape=jax.ShapeDt...]
where the time goes in v5:
time: 93.2 us; the launch traced here: 93.1 us
  Pallas kernels  91.2 us (98%)
  local copies, waits for them, and re-layouts  1.82 us (2%)
    pallas_call x1, Pallas kernels, in_planes(): pl.pallas_call(functools.partial(plane_kernel, nz), out_shape=jax.ShapeDt...  91.2 us

profile of v5, /device:TPU:0, one launch (start us, length us, event | category | flops | bytes accessed | tf_op | source)
XLA Modules:
  0.0 93.1 jit_solution(3542258300492451488)
XLA Ops:
  0.0 91.2 %shard_map.109 = bf16[64,3584]{1,0:T(8,128)(2,1)} custom-call(bf16[64,3584]{1,0:T(8,128)(2,1)} %tokens_ref.1, f32[3584]{0:T(1024)} %gain_ref.1, bf16[224,1536]{1,0:T(8,128)(2,1)} %w_query_ref.1, bf16[224,512]{1,0:T(8,128)(2,1)} %w_key_ref.1, bf16[224,512]{1,0:T(8,128)(2,1)} %w_value_ref.1, f32[1536]{0:T(1024)} %q_bias_ref.1, f32[1,512]{1,0:T(1,128)} %bitcast.4, ...), custom_call_target="tpu_custom_call" | custom-call | tf_op jit(solution)/shard_map/pallas_call | solution.py:1178
  91.2 1.8 %copy.13 = bf16[64,3584]{1,0:T(8,128)(2,1)} copy(bf16[64,3584]{1,0:T(8,128)(2,1)} %shard_map.109) | data formatting | bytes 917504
